TPU v7x, 32 devices: a whole 2x2x4 slice. The times are simulated.
32 devices in a mesh: gx: 4 (over y, x), gy: 8 (over z, core).
Axes of the slice: x: 2, y: 2, z: 4, core: 2. Of those that a mesh axis runs over, the one named last changes fastest.
Arguments:
- primal: float32 [4, 27, 16384], P(None, None, ('gx', 'gy')), may hold values from -6 to 6
- adjoint: float32 [4, 27, 16384], P(None, None, ('gx', 'gy')), may hold values from -6 to 6
- source: float32 [4, 27, 16384], P(None, None, ('gx', 'gy')), may hold values from -6 to 6
- coefficient: float32 [16384], P(('gx', 'gy')), may hold values from 0.3 to 3
- levels: int32 [16384], P(('gx', 'gy')), may hold values from 0 to 3
- recon: float32 [7, 125, 27], replicated, may hold values from -0.4375 to 0.4375
- stiffness: float32 [125, 27], replicated, may hold values from -1.25 to 1.25
- interp: float32 [125, 27], replicated, may hold values from -1.25 to 1.25
- flux: float32 [6, 25, 27], replicated, may hold values from -1.25 to 1.25
- face_eval: float32 [6, 25, 125], replicated, may hold values from -0.5 to 0.5
- child_interp: float32 [4, 25, 25], replicated, may hold values from -1.25 to 1.25
- ghost_send: int32 [32, 8, 32], P(('gx', 'gy')), may hold values from -1 to 511, as said below
- edge_send: int32 [32, 2, 16], P(('gx', 'gy')), may hold values from -1 to 511, as said below
- neighbor_slot: int32 [6, 16384], P(None, ('gx', 'gy')), may hold values from -1 to 799, as said below
- neighbor_child: int32 [6, 16384], P(None, ('gx', 'gy')), may hold values from 0 to 4, as said below
- hang_send: int32 [2, 32, 8, 8], P(None, ('gx', 'gy')), may hold values from -1 to 511, as said below
- hang_recv: int32 [3, 32, 8, 8], P(None, ('gx', 'gy')), may hold values from -1 to 511, as said below
Outputs:
- cell_indicator: float32 [4, 16384], P(None, ('gx', 'gy'))
- face_indicator: float32 [4, 16384], P(None, ('gx', 'gy'))
Inputs may be any that keep to these rules, and one draw needn't show every extreme that they name: `ghost_send`: the gy index of a device numbers a block of a cube of blocks with side S, the cube root of 8: index = G(c0) + S * G(c1) + S * S * G(c2) for block coordinates c0, c1, c2, where G(p) = p xor (p // 2) is the Gray code, so face-adjacent blocks differ in one bit of the index. Row [r, p] lists the local cells that device r sends to the device with its gx index and gy index p, live ids first, then -1. Only the up to six blocks face-adjacent to r's block get live ids, between 16 and 32 of them, and exactly 32 go to the neighbour one step up along coordinate 0 wherever it exists. `edge_send`: row [r, 0] lists the local cells sent to the device one gx index lower with the same gy index, row [r, 1] those sent to the one higher, live ids first, then -1; where that device exists there are 8 to 16 live ids, and exactly 16 towards the lower one; otherwise the row is all -1. `neighbor_slot`: every slot that is not -1 points at a live entry: a cell of the device itself, a live entry of a gy peer's ghost_send row for this device, or a live entry of a gx neighbour's edge_send row towards this device. `neighbor_child`: 4 means a neighbour of the same level. `hang_send`: [0, r, p, t] is a local cell of device r and [1, r, p, t] one of its faces, both -1 after the live slots; live slots go only to face-adjacent gy peers (as for ghost_send), at most 8 to one peer, and the device with gy index 0 sends exactly 8 to each of its face-adjacent peers. `hang_recv`: [:, q, p, t] describes what device q receives in slot t from the device with its gx index and gy index p: a local coarse cell, its face (the opposite of the sender's fine face) and a child position 0 to 3; all three are -1 exactly where the sender's slot is empty.
All inputs are finite; a program needn't handle non-finite values.
Results may differ from a plain program's by a relative error of at most 0.0003.
Values sent between devices are 32-bit elements; how exact they have to be, the bound alone decides.
A program may use at most 128 MiB of HBM per device.

v0:
```python
import functools
import math

import jax
import jax.numpy as jnp
from jax import lax
from jax.experimental import pallas as pl
from jax.experimental.pallas import tpu as pltpu
from jax.sharding import PartitionSpec as P

LANES = 128
F32 = jnp.float32
BF16 = jnp.bfloat16
MESH = pl.DeviceIdType.MESH


def round_up(value, unit):
    return -(-value // unit) * unit


def split(x):
    hi = x.astype(BF16)
    lo = (x - hi.astype(F32)).astype(BF16)
    return hi, lo


def mm(a, b):
    return jnp.dot(a, b, preferred_element_type=F32)


def dot3(a_both, b_hi, b_lo):
    rows = a_both.shape[0] // 2
    first = mm(a_both, b_hi)
    return first[:rows] + first[rows:] + mm(a_both[:rows], b_lo)


def fill_flat(flat, refs, width):
    for at, ref in enumerate(refs):
        dofs, fields, cells = ref.shape
        used = dofs * fields
        for i in range(cells // LANES):
            for j in range(dofs):
                row = at * width + j * fields
                flat[i, row : row + fields, :] = ref[j, :, i * LANES : (i + 1) * LANES]
            flat[i, at * width + used : (at + 1) * width, :] = jnp.zeros((width - used, LANES), F32)


def lane_gather(blocks, lane, block_id):
    total = jnp.zeros(blocks[0].shape, F32)
    for i, block in enumerate(blocks):
        got = jnp.take_along_axis(block, lane, axis=1)
        total = jnp.where(block_id == i, got, total)
    return total


def compute_kernel(
    dims,
    primal_ref,
    adjoint_ref,
    source_ref,
    coef_ref,
    levels_ref,
    recon_ref,
    stiffness_ref,
    interp_ref,
    flux_ref,
    face_eval_ref,
    child_interp_ref,
    slot_ref,
    child_ref,
    hang_ref,
    ghost_ref,
    edge_ref,
    hang_send_ref,
    cell_ref,
    face_ref,
    op_recon,
    op_res,
    op_face,
    op_child,
    child_flat,
    op_flux,
    op_map,
    maps,
    z_hi,
    z_lo,
    u_hi,
    u_lo,
    sources,
    flat,
    source_flat,
    hang_flat,
    near,
    residuals,
    from_gy,
    from_gx,
    to_gy,
    to_gx,
    ids,
    packed,
    send_gy,
    recv_gy,
    send_gx,
    recv_gx,
):
    n_gx, n_gy, bits, ghosts, edges, hangs, fields, rows = dims
    gx = lax.axis_index("gx")
    gy = lax.axis_index("gy")
    dofs, _, cells = primal_ref.shape
    width = fields * rows
    partners = [jnp.bitwise_xor(gy, 1 << b) for b in range(bits)]

    barrier = pltpu.get_barrier_semaphore()
    for partner in partners:
        pl.semaphore_signal(barrier, inc=1, device_id=(gx, partner), device_id_type=MESH)

    @pl.when(gx > 0)
    def _():
        pl.semaphore_signal(barrier, inc=1, device_id=(gx - 1, gy), device_id_type=MESH)

    @pl.when(gx < n_gx - 1)
    def _():
        pl.semaphore_signal(barrier, inc=1, device_id=(gx + 1, gy), device_id_type=MESH)

    main = bits * ghosts + 2 * edges
    main_pad = round_up(main, LANES)
    hang_pad = round_up(bits * hangs, LANES)
    ids[...] = jnp.zeros_like(ids)
    for b, partner in enumerate(partners):
        ids[0:1, b * ghosts : (b + 1) * ghosts] = ghost_ref[0, pl.ds(partner, 1), :]
        at = main_pad + b * hangs
        ids[0:1, at : at + hangs] = hang_send_ref[0, 0, pl.ds(partner, 1), :]
    for side in range(2):
        at = bits * ghosts + side * edges
        ids[0:1, at : at + edges] = edge_ref[0, side : side + 1, :]
    fill_flat(flat, (primal_ref, adjoint_ref), width)
    chosen = jnp.maximum(ids[0:1, :], 0)
    for at in range(0, main_pad + hang_pad, LANES):
        part = jnp.broadcast_to(chosen[:, at : at + LANES], (rows, LANES))
        lane = jnp.bitwise_and(part, LANES - 1)
        block_id = jnp.right_shift(part, 7)
        count = 2 * fields if at < main_pad else fields
        for group in range(count):
            blocks = [flat[i, group * rows : (group + 1) * rows, :] for i in range(cells // LANES)]
            packed[group * rows : (group + 1) * rows, :] = lane_gather(blocks, lane, block_id)
        if at < main_pad:
            turned = packed[...].T
            for first in range(at, min(at + LANES, main), edges):
                chunk = turned[first - at : first - at + edges]
                if first < bits * ghosts:
                    inner = first % ghosts
                    to_gy[first // ghosts, inner : inner + edges, :] = chunk
                else:
                    to_gx[(first - bits * ghosts) // edges] = chunk
        else:
            turned = packed[0:width, :].T
            for b in range(bits):
                at_slot = b * hangs - (at - main_pad)
                if 0 <= at_slot < LANES:
                    to_gy[b, ghosts : ghosts + hangs, 0:width] = turned[at_slot : at_slot + hangs]
                    to_gy[b, ghosts : ghosts + hangs, width:] = jnp.zeros(
                        (hangs, to_gy.shape[2] - width), F32
                    )

    def low_copy():
        return pltpu.make_async_remote_copy(
            src_ref=to_gx.at[0],
            dst_ref=from_gx.at[1],
            send_sem=send_gx.at[0],
            recv_sem=recv_gx.at[1],
            device_id=(gx - 1, gy),
            device_id_type=MESH,
        )

    def high_copy():
        return pltpu.make_async_remote_copy(
            src_ref=to_gx.at[1],
            dst_ref=from_gx.at[0],
            send_sem=send_gx.at[1],
            recv_sem=recv_gx.at[0],
            device_id=(gx + 1, gy),
            device_id_type=MESH,
        )

    @pl.when((gx > 0) & (gx < n_gx - 1))
    def _():
        pl.semaphore_wait(barrier, bits + 2)

    @pl.when((gx == 0) | (gx == n_gx - 1))
    def _():
        pl.semaphore_wait(barrier, bits + (1 if n_gx > 1 else 0))

    copies = []
    for b in reversed(range(bits)):
        copy = pltpu.make_async_remote_copy(
            src_ref=to_gy.at[b],
            dst_ref=from_gy.at[b],
            send_sem=send_gy.at[b],
            recv_sem=recv_gy.at[b],
            device_id=(gx, partners[b]),
            device_id_type=MESH,
        )
        copy.start()
        copies.append(copy)

    @pl.when(gx > 0)
    def _():
        low_copy().start()

    @pl.when(gx == 0)
    def _():
        from_gx[0] = jnp.zeros(from_gx.shape[1:], F32)

    @pl.when(gx < n_gx - 1)
    def _():
        high_copy().start()

    @pl.when(gx == n_gx - 1)
    def _():
        from_gx[1] = jnp.zeros(from_gx.shape[1:], F32)

    quads = recon_ref.shape[2]
    own_blocks = cells // LANES
    points = flux_ref.shape[1]
    remote = bits * ghosts + 2 * edges
    remote_pad = round_up(remote, LANES)
    hang_count = bits * hangs
    hang_pad = round_up(hang_count, LANES)
    hang_rows = round_up(hang_count, 16)
    children = 4

    op_recon[...] = jnp.zeros_like(op_recon)
    op_res[...] = jnp.zeros_like(op_res)
    op_face[...] = jnp.zeros_like(op_face)
    child_flat[...] = jnp.zeros_like(child_flat)
    op_flux[...] = jnp.zeros_like(op_flux)
    for j in range(dofs):
        op_recon[8 * j : 8 * j + 7, 0:quads] = recon_ref[j]
    op_res[0:dofs, 0:quads] = interp_ref[...]
    op_res[rows : rows + dofs, 0:quads] = stiffness_ref[...]
    for f in range(6):
        op_face[f * rows : f * rows + points, 0:quads] = face_eval_ref[f]
        op_flux[0:points, f * rows : f * rows + dofs] = flux_ref[f]
    for p in range(points):
        child_flat[children * p : children * (p + 1), 0:points] = child_interp_ref[p]
    for h in range(children):
        op_child[h * rows : (h + 1) * rows, :] = child_flat[pl.ds(h, rows, stride=children), :]
    flux_all = op_flux[...]
    flux_hi, flux_lo = split(flux_all)
    child_both = jnp.concatenate(split(op_child[...]), 0)
    mapped_ops = dot3(child_both[:, 0:rows], flux_hi, flux_lo)
    for f in range(6):
        opp = f ^ 1
        for h in range(children):
            op_map[f, :, h * rows : (h + 1) * rows] = mapped_ops[
                h * rows : (h + 1) * rows, opp * rows : (opp + 1) * rows
            ]
        op_map[f, :, 4 * rows : 5 * rows] = flux_all[:, opp * rows : (opp + 1) * rows]
        op_map[f, :, 5 * rows : 6 * rows] = flux_all[:, f * rows : (f + 1) * rows]
    recon_turned = [op_recon[pl.ds(f, rows, stride=8), :] for f in range(8)]
    recon_both = jnp.concatenate(split(jnp.concatenate(recon_turned, 0).T), 0)
    res_both = jnp.concatenate(split(op_res[...].T), 0)
    face_both = jnp.concatenate(split(op_face[...]), 0)
    flux_both = jnp.concatenate([flux_hi, flux_lo], 0)[:, 0 : 6 * rows]
    back_both = jnp.concatenate(split(op_child[...].T[0:rows]), 0)
    map_both = [jnp.concatenate(split(op_map[f]), 0) for f in range(6)]

    maps[...] = jnp.full(maps.shape, -1, jnp.int32)
    for b in range(bits):
        partner = jnp.bitwise_xor(gy, 1 << b)
        for i in range(3):
            maps[i : i + 1, b * hangs : (b + 1) * hangs] = hang_ref[i, 0, pl.ds(partner, 1), :]
    lane_face = maps[1:2, :]
    lane_child = maps[2:3, :]
    live = maps[0:1, :] >= 0
    place = jnp.where(live, maps[0:1, :] + lane_face * cells, -1).astype(F32)
    place_rows = jnp.broadcast_to(place, (LANES, hang_pad)).T[0:hang_rows, 0:1]

    fill_flat(source_flat, (source_ref,), width)
    for i in range(own_blocks):
        for group in range(2 * fields):
            first = group // fields * width + group % fields
            sources[i, group * rows : (group + 1) * rows, :] = flat[
                i, pl.ds(first, rows, stride=fields), :
            ]

    slot = slot_ref[...]
    shifted = slot - cells
    log_ghosts = ghosts.bit_length() - 1
    peer = jnp.right_shift(shifted, log_ghosts)
    within = jnp.bitwise_and(shifted, ghosts - 1)
    differing = jnp.bitwise_xor(peer, gy)
    place_of = jnp.zeros_like(slot)
    for b in range(1, bits):
        place_of = jnp.where(differing == (1 << b), b, place_of)
    slot = jnp.where(
        slot < cells,
        slot,
        jnp.where(
            shifted < n_gy * ghosts,
            cells + place_of * ghosts + within,
            slot - (n_gy - bits) * ghosts,
        ),
    )
    coef = coef_ref[...]
    for k in range(fields):
        own_u = jnp.concatenate(
            [sources[i, k * rows : (k + 1) * rows, :] for i in range(own_blocks)], 1
        )
        src_hi, src_lo = split(
            jnp.concatenate(
                [source_flat[i, pl.ds(k, rows, stride=fields), :] for i in range(own_blocks)], 1
            )
        )
        scaled_hi, scaled_lo = split(-coef * own_u)
        residuals[k] = dot3(
            res_both[:, 0 : 2 * rows],
            jnp.concatenate([src_hi, scaled_hi], 0),
            jnp.concatenate([src_lo, scaled_lo], 0),
        )

    for f in range(6):
        for at in range(0, cells, LANES):
            part = jnp.broadcast_to(slot[f : f + 1, at : at + LANES], (rows, LANES))
            lane = jnp.bitwise_and(part, LANES - 1)
            block_id = jnp.right_shift(part, 7)
            for group in range(2 * fields):
                span = slice(group * rows, (group + 1) * rows)
                blocks = [sources[i, span, :] for i in range(own_blocks)]
                near[f, at // LANES, span, :] = lane_gather(blocks, lane, block_id)

    for copy in copies:
        copy.wait()

    @pl.when(gx > 0)
    def _():
        low_copy().wait_send()
        high_copy().wait_recv()

    @pl.when(gx < n_gx - 1)
    def _():
        high_copy().wait_send()
        low_copy().wait_recv()

    parts = [from_gy[b, 0:ghosts, :] for b in range(bits)] + [from_gx[0], from_gx[1]]
    if remote_pad > remote:
        parts.append(jnp.zeros((remote_pad - remote, parts[0].shape[1]), F32))
    arrived = jnp.concatenate(parts, 0).T
    for i in range(remote_pad // LANES):
        flat[own_blocks + i] = arrived[:, i * LANES : (i + 1) * LANES]
    n_blocks = own_blocks + remote_pad // LANES
    for i in range(own_blocks, n_blocks):
        for group in range(2 * fields):
            first = group // fields * width + group % fields
            sources[i, group * rows : (group + 1) * rows, :] = flat[
                i, pl.ds(first, rows, stride=fields), :
            ]
    parts = [from_gy[b, ghosts : ghosts + hangs, 0:width] for b in range(bits)]
    parts.append(jnp.zeros((hang_pad - hang_count, width), F32))
    hang_flat[...] = jnp.concatenate(parts, 0).T

    for f in range(6):
        for at in range(0, cells, LANES):
            part = jnp.broadcast_to(slot[f : f + 1, at : at + LANES], (rows, LANES))
            lane = jnp.bitwise_and(part, LANES - 1)
            block_id = jnp.right_shift(part, 7)
            for group in range(2 * fields):
                span = slice(group * rows, (group + 1) * rows)
                total = near[f, at // LANES, span, :]
                for i in range(own_blocks, n_blocks):
                    got = jnp.take_along_axis(sources[i, span, :], lane, axis=1)
                    total = jnp.where(block_id == i, got, total)
                hi, lo = split(total)
                if group < fields:
                    u_hi[group, f, :, at : at + LANES] = hi
                    u_lo[group, f, :, at : at + LANES] = lo
                else:
                    k = group - fields
                    z_hi[k, f * rows : (f + 1) * rows, at : at + LANES] = hi
                    z_lo[k, f * rows : (f + 1) * rows, at : at + LANES] = lo

    column = lax.broadcasted_iota(jnp.int32, (hang_rows, cells), 1).astype(F32)
    place_wide = jnp.broadcast_to(place_rows, (hang_rows, cells))
    scatter = [
        jnp.where(place_wide == column + float(f * cells), 1.0, 0.0).astype(BF16) for f in range(6)
    ]
    size = jnp.exp2(-levels_ref[...].astype(F32))
    zero = jnp.zeros((rows, cells), BF16)
    child_masks = []
    for f in range(6):
        wide = jnp.broadcast_to(child_ref[f : f + 1, :], (rows, cells))
        child_masks.append([wide == h for h in range(children + 1)])

    face_wide = jnp.broadcast_to(lane_face, (rows, hang_pad))
    child_wide = jnp.broadcast_to(lane_child, (rows, hang_pad))
    fine_masks = [face_wide == (f ^ 1) for f in range(6)]
    place_masks = [child_wide == h for h in range(children)]
    hang_zero = jnp.zeros((rows, hang_pad), BF16)

    for k in range(fields):
        own_u, own_z = [
            jnp.concatenate(
                [sources[i, at * rows : (at + 1) * rows, :] for i in range(own_blocks)], 1
            )
            for at in (k, fields + k)
        ]
        own_z_hi, own_z_lo = split(own_z)
        weight = dot3(
            recon_both[:, 0 : 7 * rows],
            jnp.concatenate([own_z_hi, z_hi[k]], 0),
            jnp.concatenate([own_z_lo, z_lo[k]], 0),
        )
        residual = residuals[k]
        cell_part = jnp.sum(residual * weight, axis=0, keepdims=True)
        cell_ref[k : k + 1, :] = size * cell_part * (1.0 / math.sqrt(quads))
        w_hi, w_lo = split(weight)
        face_weight = dot3(face_both, w_hi, w_lo)

        hang_parts = split(hang_flat[pl.ds(k, rows, stride=fields), :])
        hang_hi, hang_lo = [
            jnp.concatenate([jnp.where(m, x, hang_zero) for m in fine_masks], 0) for x in hang_parts
        ]
        trace_parts = split(dot3(flux_both, hang_hi, hang_lo))
        trace_hi, trace_lo = [
            jnp.concatenate([jnp.where(m, x, hang_zero) for m in place_masks], 0)
            for x in trace_parts
        ]
        traces = dot3(back_both, trace_hi, trace_lo)
        trace_both = jnp.concatenate(split(traces), 0)[:, 0:hang_rows]

        own_u_hi, own_u_lo = split(own_u)
        product = jnp.zeros((rows, cells), F32)
        for f in range(6):
            near_hi = u_hi[k, f]
            near_lo = u_lo[k, f]
            masks = child_masks[f]
            hi = jnp.concatenate([jnp.where(m, near_hi, zero) for m in masks] + [own_u_hi], 0)
            lo = jnp.concatenate([jnp.where(m, near_lo, zero) for m in masks] + [own_u_lo], 0)
            jump = dot3(map_both[f], hi, lo)
            extra = mm(trace_both, scatter[f])
            jump = jump + extra[0:rows] + extra[rows:]
            product = product + jump * face_weight[f * rows : (f + 1) * rows]
        face_part = jnp.sum(product, axis=0, keepdims=True)
        face_ref[k : k + 1, :] = size * face_part * (1.0 / math.sqrt(6 * points))


def solution(mesh):
    n_gx, n_gy = mesh.shape["gx"], mesh.shape["gy"]
    bits = n_gy.bit_length() - 1
    vmem = pl.BlockSpec(memory_space=pltpu.VMEM)

    def shards(
        primal,
        adjoint,
        source,
        coefficient,
        levels,
        recon,
        stiffness,
        interp,
        flux,
        face_eval,
        child_interp,
        ghost_send,
        edge_send,
        neighbor_slot,
        neighbor_child,
        hang_send,
        hang_recv,
    ):
        fields, dofs, cells = primal.shape
        ghosts, edges, hangs = ghost_send.shape[2], edge_send.shape[2], hang_send.shape[3]
        rows = round_up(dofs, 32)
        quads = recon.shape[1]
        quad_rows = round_up(quads, LANES)
        dims = (n_gx, n_gy, bits, ghosts, edges, hangs, fields, rows)
        primal, adjoint, source = [x.transpose(1, 0, 2) for x in (primal, adjoint, source)]
        main_pad = round_up(bits * ghosts + 2 * edges, LANES)
        hang_pad = round_up(bits * hangs, LANES)
        wide = 2 * fields * rows
        out = jax.ShapeDtypeStruct((fields, cells), F32)
        return pl.pallas_call(
            functools.partial(compute_kernel, dims),
            out_shape=(out, out),
            in_specs=[vmem] * 17,
            out_specs=(vmem, vmem),
            scratch_shapes=[
                pltpu.VMEM((8 * rows, quad_rows), F32),
                pltpu.VMEM((LANES, quad_rows), F32),
                pltpu.VMEM((6 * rows, quad_rows), F32),
                pltpu.VMEM((4 * rows, LANES), F32),
                pltpu.VMEM((4 * rows, LANES), F32),
                pltpu.VMEM((rows, round_up(6 * rows, LANES)), F32),
                pltpu.VMEM((6, rows, 6 * rows), F32),
                pltpu.VMEM((8, hang_pad), jnp.int32),
                pltpu.VMEM((fields, 6 * rows, cells), BF16),
                pltpu.VMEM((fields, 6 * rows, cells), BF16),
                pltpu.VMEM((fields, 6, rows, cells), BF16),
                pltpu.VMEM((fields, 6, rows, cells), BF16),
                pltpu.VMEM(((cells + main_pad) // LANES, wide, LANES), F32),
                pltpu.VMEM(((cells + main_pad) // LANES, wide, LANES), F32),
                pltpu.VMEM((cells // LANES, fields * rows, LANES), F32),
                pltpu.VMEM((fields * rows, hang_pad), F32),
                pltpu.VMEM((6, cells // LANES, wide, LANES), F32),
                pltpu.VMEM((fields, quad_rows, cells), F32),
                pltpu.VMEM((bits, ghosts + hangs, wide), F32),
                pltpu.VMEM((2, edges, wide), F32),
                pltpu.VMEM((bits, ghosts + hangs, wide), F32),
                pltpu.VMEM((2, edges, wide), F32),
                pltpu.VMEM((8, main_pad + hang_pad), jnp.int32),
                pltpu.VMEM((wide, LANES), F32),
                pltpu.SemaphoreType.DMA((bits,)),
                pltpu.SemaphoreType.DMA((bits,)),
                pltpu.SemaphoreType.DMA((2,)),
                pltpu.SemaphoreType.DMA((2,)),
            ],
            compiler_params=pltpu.CompilerParams(collective_id=0, has_side_effects=True),
            name="indicators",
        )(
            primal,
            adjoint,
            source,
            coefficient.reshape(1, cells),
            levels.reshape(1, cells),
            recon.transpose(2, 0, 1),
            stiffness.T,
            interp.T,
            flux,
            face_eval,
            child_interp.transpose(1, 0, 2),
            neighbor_slot,
            neighbor_child,
            hang_recv,
            ghost_send,
            edge_send,
            hang_send,
        )

    both = ("gx", "gy")
    placed = (
        P(None, None, both),
        P(None, None, both),
        P(None, None, both),
        P(both),
        P(both),
        P(),
        P(),
        P(),
        P(),
        P(),
        P(),
        P(both, None, None),
        P(both, None, None),
        P(None, both),
        P(None, both),
        P(None, both, None, None),
        P(None, both, None, None),
    )
    return jax.shard_map(
        shards,
        mesh=mesh,
        in_specs=placed,
        out_specs=(P(None, both), P(None, both)),
        check_vma=False,
    )
```

profile of v0, /device:TPU:0, one launch (start us, length us, event | category | flops | bytes accessed | tf_op | source)
XLA Modules:
  0.0 17.6 jit_solution(3404756229690446966)
XLA Ops:
  0.6 15.0 %indicators.1 = (f32[4,512]{1,0:T(4,128)}, f32[4,512]{1,0:T(4,128)}) custom-call(f32[27,4,512]{2,1,0:T(4,128)} %bitcast.9, f32[27,4,512]{2,1,0:T(4,128)} %bitcast.10, f32[27,4,512]{2,1,0:T(4,128)} %bitcast.11, f32[1,512]{1,0:T(1,128)} %bitcast.16, s32[1,512]{1,0:T(1,128)} %bitcast.17, f32[27,7,125]{2,1,0:T(8,128)} %bitcast.12, f32[27,125]{1,0:T(8,128)} %bitcast.14, ...), custom_call_target="tpu_custom_call" | custom-call | tf_op jit(solution)/shard_map/indicators/pallas_call | solution.py:482
  15.7 0.0 copy-start
  15.7 1.3 %copy.21 = f32[4,512]{1,0:T(4,128)} copy(f32[4,512]{1,0:T(4,128)} %get-tuple-element.4) | data formatting | bytes 16384
  17.0 0.0 copy-done
  17.0 0.6 %copy.22 = f32[4,512]{1,0:T(4,128)} copy(f32[4,512]{1,0:T(4,128)S(1)} %copy-done) | data formatting | bytes 16384
Async XLA Ops:
  15.7 1.3 %copy-start = (f32[4,512]{1,0:T(4,128)S(1)}, f32[4,512]{1,0:T(4,128)}, u32[]{:S(2)}) copy-start(f32[4,512]{1,0:T(4,128)} %get-tuple-element.5) | copy-start | bytes 24580
where the time goes:
time: 17.8 us; the launch traced here: 17.6 us
  Pallas kernels  15 us (84%)
  local copies, waits for them, and re-layouts  1.9 us (11%)
  between operations  0.65 us (4%)
    pallas_call x1, Pallas kernels, shards(): pl.pallas_call(functools.partial(compute_kernel, dims), out_shape=(out, o...  15 us
    unnamed x4, local copies, waits for them, and re-layouts  1.9 us

commit v1 on v0

v1 whole, which is shorter than its diff:
```python
import functools
import math

import jax
import jax.numpy as jnp
from jax import lax
from jax.experimental import pallas as pl
from jax.experimental.pallas import tpu as pltpu
from jax.sharding import PartitionSpec as P

LANES = 128
F32 = jnp.float32
BF16 = jnp.bfloat16
MESH = pl.DeviceIdType.MESH


def round_up(value, unit):
    return -(-value // unit) * unit


def split(x):
    hi = x.astype(BF16)
    lo = (x - hi.astype(F32)).astype(BF16)
    return hi, lo


def both(x):
    return jnp.concatenate(split(x), 0)


def mm(a, b):
    return jnp.dot(a, b, preferred_element_type=F32)


def mm_nt(a, b):
    return lax.dot_general(a, b, (((1,), (1,)), ((), ())), preferred_element_type=F32)


def dot3(a_both, b_hi, b_lo, dot=mm):
    rows = a_both.shape[0] // 2
    first = dot(a_both, b_hi)
    return first[:rows] + first[rows:] + dot(a_both[:rows], b_lo)


def fill_flat(flat, refs, width):
    for at, ref in enumerate(refs):
        dofs, fields, cells = ref.shape
        used = dofs * fields
        for i in range(cells // LANES):
            for j in range(dofs):
                row = at * width + j * fields
                flat[i, row : row + fields, :] = ref[j, :, i * LANES : (i + 1) * LANES]
            flat[i, at * width + used : (at + 1) * width, :] = jnp.zeros((width - used, LANES), F32)


def lane_gather(blocks, lane, block_id):
    total = jnp.zeros(blocks[0].shape, F32)
    for i, block in enumerate(blocks):
        got = jnp.take_along_axis(block, lane, axis=1)
        total = jnp.where(block_id == i, got, total)
    return total


def one_hot(index, rows):
    parts = []
    for first in range(0, rows, 256):
        count = min(256, rows - first)
        wide = jnp.broadcast_to((index - first).astype(F32), (count, index.shape[1])).astype(BF16)
        ids = lax.broadcasted_iota(jnp.int32, wide.shape, 0).astype(F32).astype(BF16)
        parts.append(jnp.where(wide == ids, jnp.ones_like(wide), jnp.zeros_like(wide)))
    return parts[0] if len(parts) == 1 else jnp.concatenate(parts, 0)


def compute_kernel(dims, n_args, *refs):
    n_gx, n_gy, bits, ghosts, edges, hangs, fields, rows, hang_rows, chunk_lanes = dims
    hbm = refs[:n_args]
    out_ref = refs[n_args]
    local = refs[n_args + 1 : 2 * n_args + 1]
    (
        op_recon,
        op_left,
        op_flux_rows,
        op_child,
        child_flat,
        op_flux,
        op_rep,
        op_z,
        op_u,
        op_trace,
        op_back,
        maps,
        z_hi,
        z_lo,
        u_all,
        sources,
        flat,
        source_flat,
        hang_flat,
        near,
        hot,
        scatter,
        part_z,
        from_gy,
        from_gx,
        to_gy,
        to_gx,
        ids,
        packed,
        in_sems,
        send_gy,
        recv_gy,
        send_gx,
        recv_gx,
    ) = refs[2 * n_args + 1 :]
    (
        primal_ref,
        adjoint_ref,
        source_ref,
        coef_ref,
        levels_ref,
        recon_ref,
        stiffness_ref,
        interp_ref,
        flux_ref,
        face_eval_ref,
        child_interp_ref,
        slot_ref,
        child_ref,
        hang_ref,
        ghost_ref,
        edge_ref,
        hang_send_ref,
    ) = local
    gx = lax.axis_index("gx")
    gy = lax.axis_index("gy")
    dofs, _, cells = primal_ref.shape
    width = fields * rows
    wide = 2 * width
    partners = [jnp.bitwise_xor(gy, 1 << b) for b in range(bits)]

    order = [14, 15, 16, 0, 1, 11, 5, 6, 7, 8, 9, 10, 13, 12, 3, 4, 2]
    loads = [pltpu.make_async_copy(hbm[i], local[i], in_sems.at[i]) for i in range(n_args)]
    for i in order[:5]:
        loads[i].start()

    barrier = pltpu.get_barrier_semaphore()
    for partner in partners:
        pl.semaphore_signal(barrier, inc=1, device_id=(gx, partner), device_id_type=MESH)

    @pl.when(gx > 0)
    def _():
        pl.semaphore_signal(barrier, inc=1, device_id=(gx - 1, gy), device_id_type=MESH)

    @pl.when(gx < n_gx - 1)
    def _():
        pl.semaphore_signal(barrier, inc=1, device_id=(gx + 1, gy), device_id_type=MESH)

    for i in order[5:]:
        loads[i].start()
    for i in order[:5]:
        loads[i].wait()

    main = bits * ghosts + 2 * edges
    main_pad = round_up(main, LANES)
    hang_pad = round_up(bits * hangs, LANES)
    ids[...] = jnp.zeros_like(ids)
    for b, partner in enumerate(partners):
        ids[0:1, b * ghosts : (b + 1) * ghosts] = ghost_ref[0, pl.ds(partner, 1), :]
        at = main_pad + b * hangs
        ids[0:1, at : at + hangs] = hang_send_ref[0, 0, pl.ds(partner, 1), :]
    for side in range(2):
        at = bits * ghosts + side * edges
        ids[0:1, at : at + edges] = edge_ref[0, side : side + 1, :]
    fill_flat(flat, (primal_ref, adjoint_ref), width)
    chosen = jnp.maximum(ids[0:1, :], 0)
    for at in range(0, main_pad + hang_pad, LANES):
        part = jnp.broadcast_to(chosen[:, at : at + LANES], (rows, LANES))
        lane = jnp.bitwise_and(part, LANES - 1)
        block_id = jnp.right_shift(part, 7)
        count = 2 * fields if at < main_pad else fields
        for group in range(count):
            blocks = [flat[i, group * rows : (group + 1) * rows, :] for i in range(cells // LANES)]
            packed[group * rows : (group + 1) * rows, :] = lane_gather(blocks, lane, block_id)
        if at < main_pad:
            turned = packed[...].T
            for first in range(at, min(at + LANES, main), edges):
                chunk = turned[first - at : first - at + edges]
                if first < bits * ghosts:
                    inner = first % ghosts
                    to_gy[first // ghosts, inner : inner + edges, :] = chunk
                else:
                    to_gx[(first - bits * ghosts) // edges] = chunk
        else:
            turned = packed[0:width, :].T
            for b in range(bits):
                at_slot = b * hangs - (at - main_pad)
                if 0 <= at_slot < LANES:
                    to_gy[b, ghosts : ghosts + hangs, 0:width] = turned[at_slot : at_slot + hangs]
                    to_gy[b, ghosts : ghosts + hangs, width:] = jnp.zeros(
                        (hangs, to_gy.shape[2] - width), F32
                    )

    def low_copy():
        return pltpu.make_async_remote_copy(
            src_ref=to_gx.at[0],
            dst_ref=from_gx.at[1],
            send_sem=send_gx.at[0],
            recv_sem=recv_gx.at[1],
            device_id=(gx - 1, gy),
            device_id_type=MESH,
        )

    def high_copy():
        return pltpu.make_async_remote_copy(
            src_ref=to_gx.at[1],
            dst_ref=from_gx.at[0],
            send_sem=send_gx.at[1],
            recv_sem=recv_gx.at[0],
            device_id=(gx + 1, gy),
            device_id_type=MESH,
        )

    @pl.when((gx > 0) & (gx < n_gx - 1))
    def _():
        pl.semaphore_wait(barrier, bits + 2)

    @pl.when((gx == 0) | (gx == n_gx - 1))
    def _():
        pl.semaphore_wait(barrier, bits + (1 if n_gx > 1 else 0))

    copies = []
    for b in reversed(range(bits)):
        copy = pltpu.make_async_remote_copy(
            src_ref=to_gy.at[b],
            dst_ref=from_gy.at[b],
            send_sem=send_gy.at[b],
            recv_sem=recv_gy.at[b],
            device_id=(gx, partners[b]),
            device_id_type=MESH,
        )
        copy.start()
        copies.append(copy)

    @pl.when(gx > 0)
    def _():
        low_copy().start()

    @pl.when(gx == 0)
    def _():
        from_gx[0] = jnp.zeros(from_gx.shape[1:], F32)

    @pl.when(gx < n_gx - 1)
    def _():
        high_copy().start()

    @pl.when(gx == n_gx - 1)
    def _():
        from_gx[1] = jnp.zeros(from_gx.shape[1:], F32)

    quads = recon_ref.shape[2]
    own_blocks = cells // LANES
    points = flux_ref.shape[1]
    remote = bits * ghosts + 2 * edges
    remote_pad = round_up(remote, LANES)
    hang_count = bits * hangs
    children = 4

    for i in order[5:]:
        loads[i].wait()

    for i in range(own_blocks):
        for group in range(2 * fields):
            first = group // fields * width + group % fields
            sources[group * rows : (group + 1) * rows, i * LANES : (i + 1) * LANES] = flat[
                i, pl.ds(first, rows, stride=fields), :
            ]
    own_both = both(sources[...])
    slot = slot_ref[...]
    shifted = slot - cells
    log_ghosts = ghosts.bit_length() - 1
    peer = jnp.right_shift(shifted, log_ghosts)
    within = jnp.bitwise_and(shifted, ghosts - 1)
    differing = jnp.bitwise_xor(peer, gy)
    place_of = jnp.zeros_like(slot)
    for b in range(1, bits):
        place_of = jnp.where(differing == (1 << b), b, place_of)
    far = jnp.where(
        shifted < n_gy * ghosts, place_of * ghosts + within, shifted - (n_gy - bits) * ghosts
    )
    far = jnp.where(shifted < 0, -1, far)
    for f in range(6):
        for at in range(0, cells, chunk_lanes):
            cols = slice(at, at + chunk_lanes)
            got = mm(own_both, one_hot(slot[f : f + 1, cols], cells))
            near[f, :, cols] = got[:wide] + got[wide:]
    for f in range(6):
        for at in range(0, cells, chunk_lanes):
            cols = slice(at, at + chunk_lanes)
            hot_part = one_hot(far[f : f + 1, cols], remote_pad)
            hot[f, 0:remote_pad, cols] = hot_part
            hot[f, remote_pad : 2 * remote_pad, cols] = hot_part

    op_recon[...] = jnp.zeros_like(op_recon)
    op_left[...] = jnp.zeros_like(op_left)
    op_flux_rows[...] = jnp.zeros_like(op_flux_rows)
    child_flat[...] = jnp.zeros_like(child_flat)
    op_flux[...] = jnp.zeros_like(op_flux)
    for j in range(dofs):
        op_recon[8 * j : 8 * j + 7, 0:quads] = recon_ref[j]
    op_left[0:dofs, 0:quads] = interp_ref[...]
    op_left[rows : rows + dofs, 0:quads] = stiffness_ref[...]
    for f in range(6):
        at = (3 + f) * rows
        op_left[at : at + points, 0:quads] = face_eval_ref[f]
        op_flux_rows[f * rows : f * rows + points, 0:dofs] = flux_ref[f]
        op_flux[0:points, f * rows : f * rows + dofs] = flux_ref[f]
    for p in range(points):
        child_flat[children * p : children * (p + 1), 0:points] = child_interp_ref[p]
    for h in range(children):
        op_child[h * rows : (h + 1) * rows, :] = child_flat[pl.ds(h, rows, stride=children), :]
    flux_turned = op_flux_rows[...].T[0:rows]
    face_eval = op_left[3 * rows : 9 * rows, :]
    op_left[2 * rows : 3 * rows, :] = dot3(both(flux_turned), *split(face_eval))
    recon_turned = jnp.concatenate([op_recon[pl.ds(f, rows, stride=8), :] for f in range(7)], 0)
    op_z[...] = both(dot3(both(op_left[...]), *split(recon_turned), dot=mm_nt))
    for f in range(6):
        single = op_flux_rows[f * rows : (f + 1) * rows, :]
        thrice = single + pltpu.roll(single, rows, 1) + pltpu.roll(single, 2 * rows, 1)
        op_rep[:, (f ^ 1) * LANES : ((f ^ 1) + 1) * LANES] = thrice
    child_both = both(op_child[...])
    mapped_ops = dot3(child_both[:, 0:rows], *split(op_rep[...]))
    high_lanes = lax.broadcasted_iota(jnp.int32, (5 * rows, LANES), 1) < 2 * rows
    for f in range(6):
        cols = slice(f * LANES, (f + 1) * LANES)
        maps_f = jnp.concatenate([mapped_ops[:, cols], op_rep[:, cols]], 0)
        hi, lo = split(maps_f)
        op_u[f] = jnp.where(high_lanes, hi.astype(F32), lo.astype(F32)).astype(BF16)
    op_trace[...] = both(op_flux[...])
    op_back[...] = both(op_child[...].T[0:rows])

    maps[...] = jnp.full(maps.shape, -1, jnp.int32)
    for b in range(bits):
        partner = jnp.bitwise_xor(gy, 1 << b)
        for i in range(3):
            maps[i : i + 1, b * hangs : (b + 1) * hangs] = hang_ref[i, 0, pl.ds(partner, 1), :]
    live = maps[0:1, :] >= 0
    place = jnp.where(live, maps[0:1, :] + maps[1:2, :] * cells, -1).astype(F32)
    place_rows = jnp.broadcast_to(place, (LANES, hang_pad)).T[0:hang_rows, 0:1]
    column = lax.broadcasted_iota(jnp.int32, (hang_rows, cells), 1).astype(F32)
    place_wide = jnp.broadcast_to(place_rows, (hang_rows, cells))
    for f in range(6):
        hit = jnp.where(place_wide == column + float(f * cells), 1.0, 0.0).astype(BF16)
        scatter[f, 0:hang_rows] = hit
        scatter[f, hang_rows : 2 * hang_rows] = hit

    def spread(x):
        outs = []
        for first in range(0, fields * hang_rows, LANES):
            total = None
            for k in range(fields):
                at = k * hang_rows - first
                if 0 <= at < LANES:
                    piece = x[k][:, 0:LANES]
                    piece = pltpu.roll(piece, at, 1) if at else piece
                    total = piece if total is None else total + piece
            outs.append(total)
        return outs[0] if len(outs) == 1 else jnp.concatenate(outs, 1)

    maps_all = spread([maps[...] + 1] * fields) - 1
    hang_lanes = fields * hang_rows
    face_wide = jnp.broadcast_to(maps_all[1:2, :], (rows, hang_lanes))
    child_wide = jnp.broadcast_to(maps_all[2:3, :], (rows, hang_lanes))
    hang_zero = jnp.zeros((rows, hang_lanes), BF16)

    fill_flat(source_flat, (source_ref,), width)
    for k in range(fields):
        own_hi, own_lo = split(sources[(fields + k) * rows : (fields + k + 1) * rows, :])
        z_hi[k, 0:rows, :] = own_hi
        z_lo[k, 0:rows, :] = own_lo
    coef = coef_ref[...]
    size = jnp.exp2(-levels_ref[...].astype(F32))

    for copy in copies:
        copy.wait()

    @pl.when(gx > 0)
    def _():
        low_copy().wait_send()
        high_copy().wait_recv()

    @pl.when(gx < n_gx - 1)
    def _():
        high_copy().wait_send()
        low_copy().wait_recv()

    parts = [from_gy[b, 0:ghosts, :] for b in range(bits)] + [from_gx[0], from_gx[1]]
    if remote_pad > remote:
        parts.append(jnp.zeros((remote_pad - remote, parts[0].shape[1]), F32))
    arrived = jnp.concatenate(parts, 0).T
    blocks = []
    for i in range(remote_pad // LANES):
        flat[i] = arrived[:, i * LANES : (i + 1) * LANES]
        blocks.append(
            jnp.concatenate(
                [
                    flat[i, pl.ds(group // fields * width + group % fields, rows, stride=fields), :]
                    for group in range(2 * fields)
                ],
                0,
            )
        )
    halves = [split(block) for block in blocks]
    far_both = jnp.concatenate([h[0] for h in halves] + [h[1] for h in halves], 1)

    parts = [from_gy[b, ghosts : ghosts + hangs, 0:width] for b in range(bits)]
    parts.append(jnp.zeros((hang_pad - hang_count, width), F32))
    hang_flat[...] = jnp.concatenate(parts, 0).T
    live_lanes = lax.broadcasted_iota(jnp.int32, (rows, LANES), 1) < hang_rows
    hang_all = spread([hang_flat[pl.ds(k, rows, stride=fields), :] for k in range(fields)])
    hang_hi, hang_lo = [
        jnp.concatenate([jnp.where(face_wide == (f ^ 1), x, hang_zero) for f in range(6)], 0)
        for x in split(hang_all)
    ]
    trace_parts = split(dot3(op_trace[:, 0 : 6 * rows], hang_hi, hang_lo))
    trace_hi, trace_lo = [
        jnp.concatenate([jnp.where(child_wide == h, x, hang_zero) for h in range(children)], 0)
        for x in trace_parts
    ]
    lifted = dot3(op_back[...], trace_hi, trace_lo)
    lifts = []
    for k in range(fields):
        at = k * hang_rows
        block = lifted[:, at // LANES * LANES : at // LANES * LANES + LANES]
        if at % LANES:
            block = pltpu.roll(block, LANES - at % LANES, 1)
        hi, lo = split(jnp.where(live_lanes, block, 0.0))
        if 2 * hang_rows <= LANES:
            lo = pltpu.roll(lo.astype(F32), hang_rows, 1)
            lifts.append((hi.astype(F32) + lo).astype(BF16)[:, 0 : 2 * hang_rows])
        else:
            lifts.append(jnp.concatenate([hi, lo], 1))
    lift = jnp.concatenate(lifts, 0)

    for at in range(0, cells, chunk_lanes):
        cols = slice(at, at + chunk_lanes)
        for f in range(6):
            total = near[f, :, cols] + mm(far_both, hot[f, :, cols])
            hi, lo = split(total)
            for k in range(fields):
                u_rows = slice(k * rows, (k + 1) * rows)
                z_rows = slice((fields + k) * rows, (fields + k + 1) * rows)
                u_all[k, f, 0:rows, cols] = hi[u_rows]
                u_all[k, f, rows : 2 * rows, cols] = lo[u_rows]
                u_all[k, f, 2 * rows : 3 * rows, cols] = hi[u_rows]
                z_hi[k, (1 + f) * rows : (2 + f) * rows, cols] = hi[z_rows]
                z_lo[k, (1 + f) * rows : (2 + f) * rows, cols] = lo[z_rows]
        totals = []
        for k in range(fields):
            forms = dot3(op_z[...], z_hi[k, :, cols], z_lo[k, :, cols])
            own_u = sources[k * rows : (k + 1) * rows, cols]
            src = jnp.concatenate(
                [
                    source_flat[i, pl.ds(k, rows, stride=fields), :]
                    for i in range(at // LANES, (at + chunk_lanes) // LANES)
                ],
                1,
            )
            cell_part = src * forms[0:rows] - coef[:, cols] * own_u * forms[rows : 2 * rows]
            cell_sum = jnp.sum(cell_part, axis=0, keepdims=True)
            out_ref[k : k + 1, cols] = size[:, cols] * cell_sum * (1.0 / math.sqrt(quads))
            part_z[k] = forms[3 * rows :]
            totals.append(own_u * forms[2 * rows : 3 * rows])
        for f in range(6):
            child = jnp.broadcast_to(child_ref[f : f + 1, cols], (rows, chunk_lanes))
            masks = [child == h for h in range(children)]
            returned = mm(lift, scatter[f, :, cols])
            for k in range(fields):
                jumps = mm(op_u[f, :, 0 : 3 * rows], u_all[k, f, :, cols])
                jump = jumps[children * rows :]
                for h in range(children):
                    jump = jnp.where(masks[h], jumps[h * rows : (h + 1) * rows], jump)
                jump = jump + returned[k * rows : (k + 1) * rows]
                totals[k] = totals[k] + jump * part_z[k, f * rows : (f + 1) * rows]
        for k in range(fields):
            face_sum = jnp.sum(totals[k], axis=0, keepdims=True)
            row = fields + k
            out_ref[row : row + 1, cols] = size[:, cols] * face_sum * (1.0 / math.sqrt(6 * points))


def solution(mesh):
    n_gx, n_gy = mesh.shape["gx"], mesh.shape["gy"]
    bits = n_gy.bit_length() - 1

    def shards(
        primal,
        adjoint,
        source,
        coefficient,
        levels,
        recon,
        stiffness,
        interp,
        flux,
        face_eval,
        child_interp,
        ghost_send,
        edge_send,
        neighbor_slot,
        neighbor_child,
        hang_send,
        hang_recv,
    ):
        fields, dofs, cells = primal.shape
        ghosts, edges, hangs = ghost_send.shape[2], edge_send.shape[2], hang_send.shape[3]
        rows = round_up(dofs, 32)
        quads = recon.shape[1]
        quad_rows = round_up(quads, LANES)
        hang_rows = max(32, 1 << (bits * hangs - 1).bit_length())
        chunk = min(cells, 256)
        dims = (n_gx, n_gy, bits, ghosts, edges, hangs, fields, rows, hang_rows, chunk)
        primal, adjoint, source = [x.transpose(1, 0, 2) for x in (primal, adjoint, source)]
        main_pad = round_up(bits * ghosts + 2 * edges, LANES)
        hang_pad = round_up(bits * hangs, LANES)
        wide = 2 * fields * rows
        args = (
            primal,
            adjoint,
            source,
            coefficient.reshape(1, cells),
            levels.reshape(1, cells),
            recon.transpose(2, 0, 1),
            stiffness.T,
            interp.T,
            flux,
            face_eval,
            child_interp.transpose(1, 0, 2),
            neighbor_slot,
            neighbor_child,
            hang_recv,
            ghost_send,
            edge_send,
            hang_send,
        )
        raw = pl.pallas_call(
            functools.partial(compute_kernel, dims, len(args)),
            out_shape=pltpu.VMEM((2 * fields, cells), F32),
            in_specs=[pl.BlockSpec(memory_space=pltpu.MemorySpace.HBM)] * len(args),
            out_specs=pl.BlockSpec(memory_space=pltpu.VMEM),
            scratch_shapes=[pltpu.VMEM(x.shape, x.dtype) for x in args]
            + [
                pltpu.VMEM((8 * rows, quad_rows), F32),
                pltpu.VMEM((9 * rows, quad_rows), F32),
                pltpu.VMEM((6 * rows, LANES), F32),
                pltpu.VMEM((4 * rows, LANES), F32),
                pltpu.VMEM((4 * rows, LANES), F32),
                pltpu.VMEM((rows, round_up(6 * rows, LANES)), F32),
                pltpu.VMEM((rows, 6 * LANES), F32),
                pltpu.VMEM((18 * rows, 7 * rows), BF16),
                pltpu.VMEM((6, 5 * rows, LANES), BF16),
                pltpu.VMEM((2 * rows, round_up(6 * rows, LANES)), BF16),
                pltpu.VMEM((2 * rows, 4 * rows), BF16),
                pltpu.VMEM((8, hang_pad), jnp.int32),
                pltpu.VMEM((fields, 7 * rows, cells), BF16),
                pltpu.VMEM((fields, 7 * rows, cells), BF16),
                pltpu.VMEM((fields, 6, 3 * rows, cells), BF16),
                pltpu.VMEM((wide, cells), F32),
                pltpu.VMEM((max(cells, main_pad) // LANES, wide, LANES), F32),
                pltpu.VMEM((cells // LANES, fields * rows, LANES), F32),
                pltpu.VMEM((fields * rows, hang_pad), F32),
                pltpu.VMEM((6, wide, cells), F32),
                pltpu.VMEM((6, 2 * main_pad, cells), BF16),
                pltpu.VMEM((6, 2 * hang_rows, cells), BF16),
                pltpu.VMEM((fields, 6 * rows, chunk), F32),
                pltpu.VMEM((bits, ghosts + hangs, wide), F32),
                pltpu.VMEM((2, edges, wide), F32),
                pltpu.VMEM((bits, ghosts + hangs, wide), F32),
                pltpu.VMEM((2, edges, wide), F32),
                pltpu.VMEM((8, main_pad + hang_pad), jnp.int32),
                pltpu.VMEM((wide, LANES), F32),
                pltpu.SemaphoreType.DMA((len(args),)),
                pltpu.SemaphoreType.DMA((bits,)),
                pltpu.SemaphoreType.DMA((bits,)),
                pltpu.SemaphoreType.DMA((2,)),
                pltpu.SemaphoreType.DMA((2,)),
            ],
            compiler_params=pltpu.CompilerParams(collective_id=0, has_side_effects=True),
            name="indicators",
        )(*args)
        return raw[:fields], raw[fields:]

    split_all = ("gx", "gy")
    placed = (
        P(None, None, split_all),
        P(None, None, split_all),
        P(None, None, split_all),
        P(split_all),
        P(split_all),
        P(),
        P(),
        P(),
        P(),
        P(),
        P(),
        P(split_all, None, None),
        P(split_all, None, None),
        P(None, split_all),
        P(None, split_all),
        P(None, split_all, None, None),
        P(None, split_all, None, None),
    )
    return jax.shard_map(
        shards,
        mesh=mesh,
        in_specs=placed,
        out_specs=(P(None, split_all), P(None, split_all)),
        check_vma=False,
    )
```

time: 17.8 us -> 13.7 us (0.77)
  Pallas kernels: 15 us -> 12.3 us
  local copies, waits for them, and re-layouts: 1.9 us -> 0.61 us
    pallas_call x1, Pallas kernels: 15 us -> 12.3 us  [shards(): pl.pallas_call(functools.partial(compute_kernel, dims, len(args)), out_sh...]
    unnamed x4 -> x0, local copies, waits for them, and re-layouts: 1.9 us -> none
    slice x0 -> x1, local copies, waits for them, and re-layouts: none -> 0.61 us  [shards(): return (raw[:fields], raw[fields:])]
where the time goes in v1:
time: 13.7 us; the launch traced here: 13.5 us
  Pallas kernels  12.3 us (90%)
  between operations  0.65 us (5%)
  local copies, waits for them, and re-layouts  0.61 us (4%)
    pallas_call x1, Pallas kernels, shards(): pl.pallas_call(functools.partial(compute_kernel, dims, len(args)), out_sh...  12.3 us
    slice x1, local copies, waits for them, and re-layouts, shards(): return (raw[:fields], raw[fields:])  0.61 us

profile of v1, /device:TPU:0, one launch (start us, length us, event | category | flops | bytes accessed | tf_op | source)
XLA Modules:
  0.0 13.5 jit_solution(232364375095423489)
XLA Ops:
  0.6 12.3 %indicators.1 = f32[8,512]{1,0:T(8,128)S(1)} custom-call(f32[27,4,512]{2,1,0:T(4,128)} %bitcast.9, f32[27,4,512]{2,1,0:T(4,128)} %bitcast.10, f32[27,4,512]{2,1,0:T(4,128)} %bitcast.11, f32[1,512]{1,0:T(1,128)} %bitcast.16, s32[1,512]{1,0:T(1,128)} %bitcast.17, f32[27,7,125]{2,1,0:T(8,128)} %bitcast.12, f32[27,125]{1,0:T(8,128)} %bitcast.14, ...), custom_call_target="tpu_custom_call" | custom-call | tf_op jit(solution)/shard_map/indicators/pallas_call | solution.py:544
  12.9 0.6 %fusion = (f32[4,512]{1,0:T(4,128)}, f32[4,512]{1,0:T(4,128)}) fusion(f32[8,512]{1,0:T(8,128)S(1)} %indicators.1), kind=kLoop, calls=%fused_computation | loop fusion | bytes 32768 | tf_op jit(solution)/shard_map/slice | solution.py:589

commit v2 on v1

--- a/solution.py
+++ b/solution.py
@@ -12,6 +12,8 @@
 F32 = jnp.float32
 BF16 = jnp.bfloat16
 MESH = pl.DeviceIdType.MESH
+DOT_FACES = 4
+FAR_DOT_FACES = 3
 
 
 def round_up(value, unit):
@@ -80,7 +82,9 @@
         op_recon,
         op_left,
         op_flux_rows,
+        op_face_rows,
         op_child,
+        op_child_tight,
         child_flat,
         op_flux,
         op_rep,
@@ -100,10 +104,15 @@
         hot,
         scatter,
         part_z,
-        from_gy,
-        from_gx,
-        to_gy,
-        to_gx,
+        part_x,
+        from_gy_u,
+        from_gx_u,
+        from_gy_z,
+        from_gx_z,
+        to_gy_u,
+        to_gx_u,
+        to_gy_z,
+        to_gx_z,
         ids,
         packed,
         in_sems,
@@ -186,36 +195,40 @@
             for first in range(at, min(at + LANES, main), edges):
                 chunk = turned[first - at : first - at + edges]
                 if first < bits * ghosts:
-                    inner = first % ghosts
-                    to_gy[first // ghosts, inner : inner + edges, :] = chunk
+                    span = slice(first % ghosts, first % ghosts + edges)
+                    to_gy_u[first // ghosts, span, :] = chunk[:, 0:width]
+                    to_gy_z[first // ghosts, span, :] = chunk[:, width:]
                 else:
-                    to_gx[(first - bits * ghosts) // edges] = chunk
+                    side = (first - bits * ghosts) // edges
+                    to_gx_u[side] = chunk[:, 0:width]
+                    to_gx_z[side] = chunk[:, width:]
         else:
             turned = packed[0:width, :].T
             for b in range(bits):
                 at_slot = b * hangs - (at - main_pad)
                 if 0 <= at_slot < LANES:
-                    to_gy[b, ghosts : ghosts + hangs, 0:width] = turned[at_slot : at_slot + hangs]
-                    to_gy[b, ghosts : ghosts + hangs, width:] = jnp.zeros(
-                        (hangs, to_gy.shape[2] - width), F32
-                    )
-
-    def low_copy():
+                    to_gy_u[b, ghosts : ghosts + hangs, :] = turned[at_slot : at_slot + hangs]
+
+    stages = [(to_gy_z, from_gy_z, to_gx_z, from_gx_z), (to_gy_u, from_gy_u, to_gx_u, from_gx_u)]
+
+    def low_copy(stage):
+        _, _, src, dst = stages[stage]
         return pltpu.make_async_remote_copy(
-            src_ref=to_gx.at[0],
-            dst_ref=from_gx.at[1],
-            send_sem=send_gx.at[0],
-            recv_sem=recv_gx.at[1],
+            src_ref=src.at[0],
+            dst_ref=dst.at[1],
+            send_sem=send_gx.at[stage, 0],
+            recv_sem=recv_gx.at[stage, 1],
             device_id=(gx - 1, gy),
             device_id_type=MESH,
         )
 
-    def high_copy():
+    def high_copy(stage):
+        _, _, src, dst = stages[stage]
         return pltpu.make_async_remote_copy(
-            src_ref=to_gx.at[1],
-            dst_ref=from_gx.at[0],
-            send_sem=send_gx.at[1],
-            recv_sem=recv_gx.at[0],
+            src_ref=src.at[1],
+            dst_ref=dst.at[0],
+            send_sem=send_gx.at[stage, 1],
+            recv_sem=recv_gx.at[stage, 0],
             device_id=(gx + 1, gy),
             device_id_type=MESH,
         )
@@ -229,33 +242,50 @@
         pl.semaphore_wait(barrier, bits + (1 if n_gx > 1 else 0))
 
     copies = []
-    for b in reversed(range(bits)):
-        copy = pltpu.make_async_remote_copy(
-            src_ref=to_gy.at[b],
-            dst_ref=from_gy.at[b],
-            send_sem=send_gy.at[b],
-            recv_sem=recv_gy.at[b],
-            device_id=(gx, partners[b]),
-            device_id_type=MESH,
-        )
-        copy.start()
-        copies.append(copy)
-
-    @pl.when(gx > 0)
-    def _():
-        low_copy().start()
-
-    @pl.when(gx == 0)
-    def _():
-        from_gx[0] = jnp.zeros(from_gx.shape[1:], F32)
-
-    @pl.when(gx < n_gx - 1)
-    def _():
-        high_copy().start()
-
-    @pl.when(gx == n_gx - 1)
-    def _():
-        from_gx[1] = jnp.zeros(from_gx.shape[1:], F32)
+    for stage in range(2):
+        src, dst, _, far_gx = stages[stage]
+        copies.append([])
+        for b in reversed(range(bits)):
+            copy = pltpu.make_async_remote_copy(
+                src_ref=src.at[b],
+                dst_ref=dst.at[b],
+                send_sem=send_gy.at[stage, b],
+                recv_sem=recv_gy.at[stage, b],
+                device_id=(gx, partners[b]),
+                device_id_type=MESH,
+            )
+            copy.start()
+            copies[stage].append(copy)
+
+        @pl.when(gx > 0)
+        def _():
+            low_copy(stage).start()
+
+        @pl.when(gx == 0)
+        def _():
+            far_gx[0] = jnp.zeros(far_gx.shape[1:], F32)
+
+        @pl.when(gx < n_gx - 1)
+        def _():
+            high_copy(stage).start()
+
+        @pl.when(gx == n_gx - 1)
+        def _():
+            far_gx[1] = jnp.zeros(far_gx.shape[1:], F32)
+
+    def receive(stage):
+        for copy in copies[stage]:
+            copy.wait()
+
+        @pl.when(gx > 0)
+        def _():
+            low_copy(stage).wait_send()
+            high_copy(stage).wait_recv()
+
+        @pl.when(gx < n_gx - 1)
+        def _():
+            high_copy(stage).wait_send()
+            low_copy(stage).wait_recv()
 
     quads = recon_ref.shape[2]
     own_blocks = cells // LANES
@@ -264,6 +294,10 @@
     remote_pad = round_up(remote, LANES)
     hang_count = bits * hangs
     children = 4
+    tight = points // 8 * 8
+    tails = points - tight
+    form_rows = op_z.shape[0] // 2
+    tail_at = 5 * tight
 
     for i in order[5:]:
         loads[i].wait()
@@ -288,12 +322,22 @@
         shifted < n_gy * ghosts, place_of * ghosts + within, shifted - (n_gy - bits) * ghosts
     )
     far = jnp.where(shifted < 0, -1, far)
-    for f in range(6):
+    for f in range(DOT_FACES):
         for at in range(0, cells, chunk_lanes):
             cols = slice(at, at + chunk_lanes)
             got = mm(own_both, one_hot(slot[f : f + 1, cols], cells))
             near[f, :, cols] = got[:wide] + got[wide:]
-    for f in range(6):
+    for f in range(DOT_FACES, 6):
+        for at in range(0, cells, LANES):
+            cols = slice(at, at + LANES)
+            part = jnp.broadcast_to(slot[f : f + 1, cols], (rows, LANES))
+            lane = jnp.bitwise_and(part, LANES - 1)
+            block_id = jnp.right_shift(part, 7)
+            for group in range(2 * fields):
+                span = slice(group * rows, (group + 1) * rows)
+                blocks = [sources[span, i * LANES : (i + 1) * LANES] for i in range(own_blocks)]
+                near[f, span, cols] = lane_gather(blocks, lane, block_id)
+    for f in range(FAR_DOT_FACES):
         for at in range(0, cells, chunk_lanes):
             cols = slice(at, at + chunk_lanes)
             hot_part = one_hot(far[f : f + 1, cols], remote_pad)
@@ -303,6 +347,8 @@
     op_recon[...] = jnp.zeros_like(op_recon)
     op_left[...] = jnp.zeros_like(op_left)
     op_flux_rows[...] = jnp.zeros_like(op_flux_rows)
+    op_face_rows[...] = jnp.zeros_like(op_face_rows)
+    op_child_tight[...] = jnp.zeros_like(op_child_tight)
     child_flat[...] = jnp.zeros_like(child_flat)
     op_flux[...] = jnp.zeros_like(op_flux)
     for j in range(dofs):
@@ -310,8 +356,12 @@
     op_left[0:dofs, 0:quads] = interp_ref[...]
     op_left[rows : rows + dofs, 0:quads] = stiffness_ref[...]
     for f in range(6):
-        at = (3 + f) * rows
-        op_left[at : at + points, 0:quads] = face_eval_ref[f]
+        at = 3 * rows + f * tight
+        op_left[at : at + tight, 0:quads] = face_eval_ref[f, 0:tight, :]
+        for e in range(points - tight):
+            at = 3 * rows + 6 * tight + 8 * e + f
+            op_left[at : at + 1, 0:quads] = face_eval_ref[f, tight + e : tight + e + 1, :]
+        op_face_rows[f * rows : f * rows + points, 0:quads] = face_eval_ref[f]
         op_flux_rows[f * rows : f * rows + points, 0:dofs] = flux_ref[f]
         op_flux[0:points, f * rows : f * rows + dofs] = flux_ref[f]
     for p in range(points):
@@ -319,21 +369,31 @@
     for h in range(children):
         op_child[h * rows : (h + 1) * rows, :] = child_flat[pl.ds(h, rows, stride=children), :]
     flux_turned = op_flux_rows[...].T[0:rows]
-    face_eval = op_left[3 * rows : 9 * rows, :]
-    op_left[2 * rows : 3 * rows, :] = dot3(both(flux_turned), *split(face_eval))
+    op_left[2 * rows : 3 * rows, :] = dot3(both(flux_turned), *split(op_face_rows[...]))
     recon_turned = jnp.concatenate([op_recon[pl.ds(f, rows, stride=8), :] for f in range(7)], 0)
     op_z[...] = both(dot3(both(op_left[...]), *split(recon_turned), dot=mm_nt))
     for f in range(6):
         single = op_flux_rows[f * rows : (f + 1) * rows, :]
         thrice = single + pltpu.roll(single, rows, 1) + pltpu.roll(single, 2 * rows, 1)
         op_rep[:, (f ^ 1) * LANES : ((f ^ 1) + 1) * LANES] = thrice
-    child_both = both(op_child[...])
-    mapped_ops = dot3(child_both[:, 0:rows], *split(op_rep[...]))
-    high_lanes = lax.broadcasted_iota(jnp.int32, (5 * rows, LANES), 1) < 2 * rows
+    for h in range(children):
+        op_child_tight[h * tight : (h + 1) * tight, :] = op_child[h * rows : h * rows + tight, :]
+        for e in range(tails):
+            at = tail_at + 8 * e + h
+            op_child_tight[at : at + 1, :] = op_child[h * rows + tight + e : h * rows + tight + e + 1, :]
+    same = (tight, LANES)
+    op_child_tight[children * tight : 5 * tight, :] = jnp.where(
+        lax.broadcasted_iota(jnp.int32, same, 0) == lax.broadcasted_iota(jnp.int32, same, 1), 1.0, 0.0
+    )
+    for e in range(tails):
+        at = tail_at + 8 * e + children
+        op_child_tight[at : at + 1, :] = jnp.where(
+            lax.broadcasted_iota(jnp.int32, (1, LANES), 1) == tight + e, 1.0, 0.0
+        )
+    mapped_ops = dot3(both(op_child_tight[...])[:, 0:rows], *split(op_rep[...]))
+    high_lanes = lax.broadcasted_iota(jnp.int32, (op_u.shape[1], LANES), 1) < 2 * rows
     for f in range(6):
-        cols = slice(f * LANES, (f + 1) * LANES)
-        maps_f = jnp.concatenate([mapped_ops[:, cols], op_rep[:, cols]], 0)
-        hi, lo = split(maps_f)
+        hi, lo = split(mapped_ops[:, f * LANES : (f + 1) * LANES])
         op_u[f] = jnp.where(high_lanes, hi.astype(F32), lo.astype(F32)).astype(BF16)
     op_trace[...] = both(op_flux[...])
     op_back[...] = both(op_child[...].T[0:rows])
@@ -380,39 +440,60 @@
     coef = coef_ref[...]
     size = jnp.exp2(-levels_ref[...].astype(F32))
 
-    for copy in copies:
-        copy.wait()
-
-    @pl.when(gx > 0)
-    def _():
-        low_copy().wait_send()
-        high_copy().wait_recv()
-
-    @pl.when(gx < n_gx - 1)
-    def _():
-        high_copy().wait_send()
-        low_copy().wait_recv()
-
-    parts = [from_gy[b, 0:ghosts, :] for b in range(bits)] + [from_gx[0], from_gx[1]]
-    if remote_pad > remote:
-        parts.append(jnp.zeros((remote_pad - remote, parts[0].shape[1]), F32))
-    arrived = jnp.concatenate(parts, 0).T
-    blocks = []
-    for i in range(remote_pad // LANES):
-        flat[i] = arrived[:, i * LANES : (i + 1) * LANES]
-        blocks.append(
-            jnp.concatenate(
-                [
-                    flat[i, pl.ds(group // fields * width + group % fields, rows, stride=fields), :]
-                    for group in range(2 * fields)
-                ],
-                0,
+    far_lane = jnp.bitwise_and(far, LANES - 1)
+    far_block = jnp.right_shift(far, 7)
+
+    def turn(from_gy, from_gx):
+        parts = [from_gy[b, 0:ghosts, :] for b in range(bits)] + [from_gx[0], from_gx[1]]
+        if remote_pad > remote:
+            parts.append(jnp.zeros((remote_pad - remote, width), F32))
+        arrived = jnp.concatenate(parts, 0).T
+        blocks = []
+        for i in range(remote_pad // LANES):
+            flat[i, 0:width, :] = arrived[:, i * LANES : (i + 1) * LANES]
+            blocks.append(
+                jnp.concatenate(
+                    [flat[i, pl.ds(k, rows, stride=fields), :] for k in range(fields)], 0
+                )
             )
-        )
-    halves = [split(block) for block in blocks]
+        return blocks
+
+    def far_gather(blocks, base, f, at):
+        cols = slice(at, at + LANES)
+        lane = jnp.broadcast_to(far_lane[f : f + 1, cols], (rows, LANES))
+        block_id = jnp.broadcast_to(far_block[f : f + 1, cols], (rows, LANES))
+        outs = []
+        for k in range(fields):
+            span = slice(base + k * rows, base + (k + 1) * rows)
+            total = near[f, span, cols]
+            for i, block in enumerate(blocks):
+                got = jnp.take_along_axis(block[k * rows : (k + 1) * rows], lane, axis=1)
+                total = jnp.where(block_id == i, got, total)
+            outs.append(total)
+        return jnp.concatenate(outs, 0)
+
+    def put_z(f, cols, total):
+        hi, lo = split(total)
+        for k in range(fields):
+            span = slice(k * rows, (k + 1) * rows)
+            z_hi[k, (1 + f) * rows : (2 + f) * rows, cols] = hi[span]
+            z_lo[k, (1 + f) * rows : (2 + f) * rows, cols] = lo[span]
+
+    receive(0)
+    blocks_z = turn(from_gy_z, from_gx_z)
+    halves = [split(block) for block in blocks_z]
     far_both = jnp.concatenate([h[0] for h in halves] + [h[1] for h in halves], 1)
-
-    parts = [from_gy[b, ghosts : ghosts + hangs, 0:width] for b in range(bits)]
+    for f in range(FAR_DOT_FACES):
+        for at in range(0, cells, chunk_lanes):
+            cols = slice(at, at + chunk_lanes)
+            put_z(f, cols, near[f, width:, cols] + mm(far_both, hot[f, :, cols]))
+    for f in range(FAR_DOT_FACES, 6):
+        for at in range(0, cells, LANES):
+            put_z(f, slice(at, at + LANES), far_gather(blocks_z, width, f, at))
+
+    receive(1)
+    blocks_u = turn(from_gy_u, from_gx_u)
+    parts = [from_gy_u[b, ghosts : ghosts + hangs, :] for b in range(bits)]
     parts.append(jnp.zeros((hang_pad - hang_count, width), F32))
     hang_flat[...] = jnp.concatenate(parts, 0).T
     live_lanes = lax.broadcasted_iota(jnp.int32, (rows, LANES), 1) < hang_rows
@@ -427,34 +508,35 @@
         for x in trace_parts
     ]
     lifted = dot3(op_back[...], trace_hi, trace_lo)
-    lifts = []
+    mains, ends = [], []
     for k in range(fields):
         at = k * hang_rows
         block = lifted[:, at // LANES * LANES : at // LANES * LANES + LANES]
         if at % LANES:
             block = pltpu.roll(block, LANES - at % LANES, 1)
-        hi, lo = split(jnp.where(live_lanes, block, 0.0))
-        if 2 * hang_rows <= LANES:
-            lo = pltpu.roll(lo.astype(F32), hang_rows, 1)
-            lifts.append((hi.astype(F32) + lo).astype(BF16)[:, 0 : 2 * hang_rows])
-        else:
-            lifts.append(jnp.concatenate([hi, lo], 1))
-    lift = jnp.concatenate(lifts, 0)
-
+        block = jnp.where(live_lanes, block, 0.0)
+        mains.append(block[0:tight])
+        ends.append(block[tight:rows])
+    lift_hi, lift_lo = split(jnp.concatenate(mains + ends, 0))
+    if 2 * hang_rows <= LANES:
+        lift_lo = pltpu.roll(lift_lo.astype(F32), hang_rows, 1)
+        lift = (lift_hi.astype(F32) + lift_lo).astype(BF16)[:, 0 : 2 * hang_rows]
+    else:
+        lift = jnp.concatenate([lift_hi[:, 0:hang_rows], lift_lo[:, 0:hang_rows]], 1)
+    end_rows = rows - tight
+
+    for f in range(6):
+        for at in range(0, cells, LANES):
+            cols = slice(at, at + LANES)
+            hi, lo = split(far_gather(blocks_u, 0, f, at))
+            for k in range(fields):
+                span = slice(k * rows, (k + 1) * rows)
+                u_all[k, f, 0:rows, cols] = hi[span]
+                u_all[k, f, rows : 2 * rows, cols] = lo[span]
+                u_all[k, f, 2 * rows : 3 * rows, cols] = hi[span]
     for at in range(0, cells, chunk_lanes):
         cols = slice(at, at + chunk_lanes)
-        for f in range(6):
-            total = near[f, :, cols] + mm(far_both, hot[f, :, cols])
-            hi, lo = split(total)
-            for k in range(fields):
-                u_rows = slice(k * rows, (k + 1) * rows)
-                z_rows = slice((fields + k) * rows, (fields + k + 1) * rows)
-                u_all[k, f, 0:rows, cols] = hi[u_rows]
-                u_all[k, f, rows : 2 * rows, cols] = lo[u_rows]
-                u_all[k, f, 2 * rows : 3 * rows, cols] = hi[u_rows]
-                z_hi[k, (1 + f) * rows : (2 + f) * rows, cols] = hi[z_rows]
-                z_lo[k, (1 + f) * rows : (2 + f) * rows, cols] = lo[z_rows]
-        totals = []
+        totals, end_totals = [], []
         for k in range(fields):
             forms = dot3(op_z[...], z_hi[k, :, cols], z_lo[k, :, cols])
             own_u = sources[k * rows : (k + 1) * rows, cols]
@@ -468,21 +550,35 @@
             cell_part = src * forms[0:rows] - coef[:, cols] * own_u * forms[rows : 2 * rows]
             cell_sum = jnp.sum(cell_part, axis=0, keepdims=True)
             out_ref[k : k + 1, cols] = size[:, cols] * cell_sum * (1.0 / math.sqrt(quads))
-            part_z[k] = forms[3 * rows :]
-            totals.append(own_u * forms[2 * rows : 3 * rows])
+            part_z[k] = forms[3 * rows : 3 * rows + 6 * tight]
+            part_x[k] = forms[3 * rows + 6 * tight : 3 * rows + 6 * tight + 8 * tails]
+            own_part = own_u * forms[2 * rows : 3 * rows]
+            end_totals.append(sum(own_part[i : i + 8] for i in range(8, rows, 8)) + own_part[0:8])
+            totals.append(jnp.zeros((tight, chunk_lanes), F32))
         for f in range(6):
-            child = jnp.broadcast_to(child_ref[f : f + 1, cols], (rows, chunk_lanes))
+            child = jnp.broadcast_to(child_ref[f : f + 1, cols], (tight, chunk_lanes))
             masks = [child == h for h in range(children)]
+            sub = lax.broadcasted_iota(jnp.int32, (8, chunk_lanes), 0)
+            end_mask = sub == child[0:8]
             returned = mm(lift, scatter[f, :, cols])
             for k in range(fields):
                 jumps = mm(op_u[f, :, 0 : 3 * rows], u_all[k, f, :, cols])
-                jump = jumps[children * rows :]
+                jump = jumps[children * tight : 5 * tight]
                 for h in range(children):
-                    jump = jnp.where(masks[h], jumps[h * rows : (h + 1) * rows], jump)
-                jump = jump + returned[k * rows : (k + 1) * rows]
-                totals[k] = totals[k] + jump * part_z[k, f * rows : (f + 1) * rows]
+                    jump = jnp.where(masks[h], jumps[h * tight : (h + 1) * tight], jump)
+                jump = jump + returned[k * tight : (k + 1) * tight]
+                totals[k] = totals[k] + jump * part_z[k, f * tight : (f + 1) * tight]
+                end_at = fields * tight + k * end_rows
+                for e in range(tails):
+                    block = jumps[tail_at + 8 * e : tail_at + 8 * (e + 1)]
+                    back = returned[end_at + 8 * (e // 8) : end_at + 8 * (e // 8) + 8]
+                    if tails > 1:
+                        back = jnp.where(sub == e % 8, back, 0.0)
+                    block = jnp.where(end_mask, block, 0.0) + back
+                    weight = jnp.broadcast_to(part_x[k, 8 * e + f : 8 * e + f + 1, :], block.shape)
+                    end_totals[k] = end_totals[k] + block * weight
         for k in range(fields):
-            face_sum = jnp.sum(totals[k], axis=0, keepdims=True)
+            face_sum = jnp.sum(jnp.concatenate([totals[k], end_totals[k]], 0), axis=0, keepdims=True)
             row = fields + k
             out_ref[row : row + 1, cols] = size[:, cols] * face_sum * (1.0 / math.sqrt(6 * points))
 
@@ -522,6 +618,10 @@
         main_pad = round_up(bits * ghosts + 2 * edges, LANES)
         hang_pad = round_up(bits * hangs, LANES)
         wide = 2 * fields * rows
+        points = flux.shape[1]
+        tight, tails = points // 8 * 8, points % 8
+        form_rows = round_up(3 * rows + 6 * tight + 8 * tails, 16)
+        map_rows = round_up(5 * tight + 8 * tails, 16)
         args = (
             primal,
             adjoint,
@@ -549,14 +649,16 @@
             scratch_shapes=[pltpu.VMEM(x.shape, x.dtype) for x in args]
             + [
                 pltpu.VMEM((8 * rows, quad_rows), F32),
-                pltpu.VMEM((9 * rows, quad_rows), F32),
+                pltpu.VMEM((form_rows, quad_rows), F32),
                 pltpu.VMEM((6 * rows, LANES), F32),
+                pltpu.VMEM((6 * rows, quad_rows), F32),
                 pltpu.VMEM((4 * rows, LANES), F32),
+                pltpu.VMEM((map_rows, LANES), F32),
                 pltpu.VMEM((4 * rows, LANES), F32),
                 pltpu.VMEM((rows, round_up(6 * rows, LANES)), F32),
                 pltpu.VMEM((rows, 6 * LANES), F32),
-                pltpu.VMEM((18 * rows, 7 * rows), BF16),
-                pltpu.VMEM((6, 5 * rows, LANES), BF16),
+                pltpu.VMEM((2 * form_rows, 7 * rows), BF16),
+                pltpu.VMEM((6, map_rows, LANES), BF16),
                 pltpu.VMEM((2 * rows, round_up(6 * rows, LANES)), BF16),
                 pltpu.VMEM((2 * rows, 4 * rows), BF16),
                 pltpu.VMEM((8, hang_pad), jnp.int32),
@@ -570,18 +672,24 @@
                 pltpu.VMEM((6, wide, cells), F32),
                 pltpu.VMEM((6, 2 * main_pad, cells), BF16),
                 pltpu.VMEM((6, 2 * hang_rows, cells), BF16),
-                pltpu.VMEM((fields, 6 * rows, chunk), F32),
-                pltpu.VMEM((bits, ghosts + hangs, wide), F32),
-                pltpu.VMEM((2, edges, wide), F32),
-                pltpu.VMEM((bits, ghosts + hangs, wide), F32),
-                pltpu.VMEM((2, edges, wide), F32),
+                pltpu.VMEM((fields, 6 * tight, chunk), F32),
+                pltpu.VMEM((fields, max(8 * tails, 8), chunk), F32),
+            ]
+            + [
+                pltpu.VMEM((bits, ghosts + hangs, wide // 2), F32),
+                pltpu.VMEM((2, edges, wide // 2), F32),
+                pltpu.VMEM((bits, ghosts, wide // 2), F32),
+                pltpu.VMEM((2, edges, wide // 2), F32),
+            ]
+            * 2
+            + [
                 pltpu.VMEM((8, main_pad + hang_pad), jnp.int32),
                 pltpu.VMEM((wide, LANES), F32),
                 pltpu.SemaphoreType.DMA((len(args),)),
-                pltpu.SemaphoreType.DMA((bits,)),
-                pltpu.SemaphoreType.DMA((bits,)),
-                pltpu.SemaphoreType.DMA((2,)),
-                pltpu.SemaphoreType.DMA((2,)),
+                pltpu.SemaphoreType.DMA((2, bits)),
+                pltpu.SemaphoreType.DMA((2, bits)),
+                pltpu.SemaphoreType.DMA((2, 2)),
+                pltpu.SemaphoreType.DMA((2, 2)),
             ],
             compiler_params=pltpu.CompilerParams(collective_id=0, has_side_effects=True),
             name="indicators",

time: 13.7 us -> 12.5 us (0.912)
  Pallas kernels: 12.3 us -> 11 us
    pallas_call x1, Pallas kernels: 12.3 us -> 11 us  [shards(): pl.pallas_call(functools.partial(compute_kernel, dims, len(args)), out_sh...]
where the time goes in v2:
time: 12.5 us; the launch traced here: 12.3 us
  Pallas kernels  11 us (88%)
  between operations  0.65 us (5%)
  local copies, waits for them, and re-layouts  0.61 us (5%)
    pallas_call x1, Pallas kernels, shards(): pl.pallas_call(functools.partial(compute_kernel, dims, len(args)), out_sh...  11 us
    slice x1, local copies, waits for them, and re-layouts, shards(): return (raw[:fields], raw[fields:])  0.61 us

profile of v2, /device:TPU:0, one launch (start us, length us, event | category | flops | bytes accessed | tf_op | source)
XLA Modules:
  0.0 12.3 jit_solution(9022045514113254261)
XLA Ops:
  0.6 11.0 %indicators.1 = f32[8,512]{1,0:T(8,128)S(1)} custom-call(f32[27,4,512]{2,1,0:T(4,128)} %bitcast.9, f32[27,4,512]{2,1,0:T(4,128)} %bitcast.10, f32[27,4,512]{2,1,0:T(4,128)} %bitcast.11, f32[1,512]{1,0:T(1,128)} %bitcast.16, s32[1,512]{1,0:T(1,128)} %bitcast.17, f32[27,7,125]{2,1,0:T(8,128)} %bitcast.12, f32[27,125]{1,0:T(8,128)} %bitcast.14, ...), custom_call_target="tpu_custom_call" | custom-call | tf_op jit(solution)/shard_map/indicators/pallas_call | solution.py:644
  11.7 0.6 %fusion = (f32[4,512]{1,0:T(4,128)}, f32[4,512]{1,0:T(4,128)}) fusion(f32[8,512]{1,0:T(8,128)S(1)} %indicators.1), kind=kLoop, calls=%fused_computation | loop fusion | bytes 32768 | tf_op jit(solution)/shard_map/slice | solution.py:697

commit v3 on v2

--- a/solution.py
+++ b/solution.py
@@ -44,15 +44,14 @@
     return first[:rows] + first[rows:] + dot(a_both[:rows], b_lo)
 
 
-def fill_flat(flat, refs, width):
-    for at, ref in enumerate(refs):
-        dofs, fields, cells = ref.shape
-        used = dofs * fields
-        for i in range(cells // LANES):
-            for j in range(dofs):
-                row = at * width + j * fields
-                flat[i, row : row + fields, :] = ref[j, :, i * LANES : (i + 1) * LANES]
-            flat[i, at * width + used : (at + 1) * width, :] = jnp.zeros((width - used, LANES), F32)
+def fill_flat(flat, ref, base, width):
+    dofs, fields, cells = ref.shape
+    used = dofs * fields
+    for i in range(cells // LANES):
+        for j in range(dofs):
+            row = base + j * fields
+            flat[i, row : row + fields, :] = ref[j, :, i * LANES : (i + 1) * LANES]
+        flat[i, base + used : base + width, :] = jnp.zeros((width - used, LANES), F32)
 
 
 def lane_gather(blocks, lane, block_id):
@@ -120,6 +119,7 @@
         recv_gy,
         send_gx,
         recv_gx,
+        ready,
     ) = refs[2 * n_args + 1 :]
     (
         primal_ref,
@@ -147,32 +147,31 @@
     wide = 2 * width
     partners = [jnp.bitwise_xor(gy, 1 << b) for b in range(bits)]
 
-    order = [14, 15, 16, 0, 1, 11, 5, 6, 7, 8, 9, 10, 13, 12, 3, 4, 2]
+    bit_of = [gy // (1 << b) % 2 for b in range(bits)]
+    barrier = pltpu.get_barrier_semaphore()
+    for b, partner in enumerate(partners):
+
+        @pl.when(bit_of[b] == 0)
+        def _():
+            pl.semaphore_signal(barrier, inc=1, device_id=(gx, partner), device_id_type=MESH)
+
+    @pl.when(gx < n_gx - 1)
+    def _():
+        pl.semaphore_signal(barrier, inc=1, device_id=(gx + 1, gy), device_id_type=MESH)
+
+    order = [14, 15, 16, 1, 0, 11, 5, 6, 7, 8, 9, 10, 13, 12, 3, 4, 2]
     loads = [pltpu.make_async_copy(hbm[i], local[i], in_sems.at[i]) for i in range(n_args)]
     for i in order[:5]:
         loads[i].start()
-
-    barrier = pltpu.get_barrier_semaphore()
-    for partner in partners:
-        pl.semaphore_signal(barrier, inc=1, device_id=(gx, partner), device_id_type=MESH)
-
-    @pl.when(gx > 0)
-    def _():
-        pl.semaphore_signal(barrier, inc=1, device_id=(gx - 1, gy), device_id_type=MESH)
-
-    @pl.when(gx < n_gx - 1)
-    def _():
-        pl.semaphore_signal(barrier, inc=1, device_id=(gx + 1, gy), device_id_type=MESH)
-
-    for i in order[5:]:
-        loads[i].start()
-    for i in order[:5]:
-        loads[i].wait()
 
     main = bits * ghosts + 2 * edges
     main_pad = round_up(main, LANES)
     hang_pad = round_up(bits * hangs, LANES)
     ids[...] = jnp.zeros_like(ids)
+    for i in order[:4]:
+        loads[i].wait()
+    for i in order[5:]:
+        loads[i].start()
     for b, partner in enumerate(partners):
         ids[0:1, b * ghosts : (b + 1) * ghosts] = ghost_ref[0, pl.ds(partner, 1), :]
         at = main_pad + b * hangs
@@ -180,36 +179,56 @@
     for side in range(2):
         at = bits * ghosts + side * edges
         ids[0:1, at : at + edges] = edge_ref[0, side : side + 1, :]
-    fill_flat(flat, (primal_ref, adjoint_ref), width)
     chosen = jnp.maximum(ids[0:1, :], 0)
-    for at in range(0, main_pad + hang_pad, LANES):
+
+    lower = sum(bit_of) + jnp.minimum(gx, 1)
+
+    @pl.when(lower > 0)
+    def _():
+        pl.semaphore_wait(barrier, lower)
+
+    for b, partner in enumerate(partners):
+
+        @pl.when(bit_of[b] == 1)
+        def _():
+            pl.semaphore_signal(ready.at[b], inc=1, device_id=(gx, partner), device_id_type=MESH)
+
+    @pl.when(gx > 0)
+    def _():
+        pl.semaphore_signal(ready.at[bits], inc=1, device_id=(gx - 1, gy), device_id_type=MESH)
+
+    def pick(base, at):
         part = jnp.broadcast_to(chosen[:, at : at + LANES], (rows, LANES))
         lane = jnp.bitwise_and(part, LANES - 1)
         block_id = jnp.right_shift(part, 7)
-        count = 2 * fields if at < main_pad else fields
-        for group in range(count):
-            blocks = [flat[i, group * rows : (group + 1) * rows, :] for i in range(cells // LANES)]
-            packed[group * rows : (group + 1) * rows, :] = lane_gather(blocks, lane, block_id)
-        if at < main_pad:
-            turned = packed[...].T
+        for k in range(fields):
+            span = slice(base + k * rows, base + (k + 1) * rows)
+            blocks = [flat[i, span, :] for i in range(cells // LANES)]
+            packed[span, :] = lane_gather(blocks, lane, block_id)
+        return packed[base : base + width, :].T
+
+    def pack(base, to_gy, to_gx):
+        for at in range(0, main_pad, LANES):
+            turned = pick(base, at)
             for first in range(at, min(at + LANES, main), edges):
                 chunk = turned[first - at : first - at + edges]
                 if first < bits * ghosts:
-                    span = slice(first % ghosts, first % ghosts + edges)
-                    to_gy_u[first // ghosts, span, :] = chunk[:, 0:width]
-                    to_gy_z[first // ghosts, span, :] = chunk[:, width:]
+                    to_gy[first // ghosts, pl.ds(first % ghosts, edges), :] = chunk
                 else:
-                    side = (first - bits * ghosts) // edges
-                    to_gx_u[side] = chunk[:, 0:width]
-                    to_gx_z[side] = chunk[:, width:]
-        else:
-            turned = packed[0:width, :].T
-            for b in range(bits):
-                at_slot = b * hangs - (at - main_pad)
-                if 0 <= at_slot < LANES:
-                    to_gy_u[b, ghosts : ghosts + hangs, :] = turned[at_slot : at_slot + hangs]
+                    to_gx[(first - bits * ghosts) // edges] = chunk
 
     stages = [(to_gy_z, from_gy_z, to_gx_z, from_gx_z), (to_gy_u, from_gy_u, to_gx_u, from_gx_u)]
+
+    def gy_copy(stage, b):
+        src, dst, _, _ = stages[stage]
+        return pltpu.make_async_remote_copy(
+            src_ref=src.at[b],
+            dst_ref=dst.at[b],
+            send_sem=send_gy.at[stage, b],
+            recv_sem=recv_gy.at[stage, b],
+            device_id=(gx, partners[b]),
+            device_id_type=MESH,
+        )
 
     def low_copy(stage):
         _, _, src, dst = stages[stage]
@@ -233,49 +252,58 @@
             device_id_type=MESH,
         )
 
-    @pl.when((gx > 0) & (gx < n_gx - 1))
-    def _():
-        pl.semaphore_wait(barrier, bits + 2)
-
-    @pl.when((gx == 0) | (gx == n_gx - 1))
-    def _():
-        pl.semaphore_wait(barrier, bits + (1 if n_gx > 1 else 0))
-
-    copies = []
-    for stage in range(2):
-        src, dst, _, far_gx = stages[stage]
-        copies.append([])
+    def send_lower(stage):
         for b in reversed(range(bits)):
-            copy = pltpu.make_async_remote_copy(
-                src_ref=src.at[b],
-                dst_ref=dst.at[b],
-                send_sem=send_gy.at[stage, b],
-                recv_sem=recv_gy.at[stage, b],
-                device_id=(gx, partners[b]),
-                device_id_type=MESH,
-            )
-            copy.start()
-            copies[stage].append(copy)
+
+            @pl.when(bit_of[b] == 1)
+            def _():
+                gy_copy(stage, b).start()
 
         @pl.when(gx > 0)
         def _():
             low_copy(stage).start()
 
-        @pl.when(gx == 0)
+    fill_flat(flat, adjoint_ref, width, width)
+    pack(width, to_gy_z, to_gx_z)
+    send_lower(0)
+    loads[order[4]].wait()
+    fill_flat(flat, primal_ref, 0, width)
+    pack(0, to_gy_u, to_gx_u)
+    for at in range(main_pad, main_pad + hang_pad, LANES):
+        turned = pick(0, at)
+        for b in range(bits):
+            at_slot = b * hangs - (at - main_pad)
+            if 0 <= at_slot < LANES:
+                to_gy_u[b, ghosts : ghosts + hangs, :] = turned[at_slot : at_slot + hangs]
+    send_lower(1)
+
+    for b in range(bits):
+
+        @pl.when(bit_of[b] == 0)
         def _():
-            far_gx[0] = jnp.zeros(far_gx.shape[1:], F32)
-
-        @pl.when(gx < n_gx - 1)
-        def _():
+            pl.semaphore_wait(ready.at[b], 1)
+            for stage in range(2):
+                gy_copy(stage, b).start()
+
+    @pl.when(gx < n_gx - 1)
+    def _():
+        pl.semaphore_wait(ready.at[bits], 1)
+        for stage in range(2):
             high_copy(stage).start()
 
-        @pl.when(gx == n_gx - 1)
-        def _():
-            far_gx[1] = jnp.zeros(far_gx.shape[1:], F32)
+    @pl.when(gx == 0)
+    def _():
+        from_gx_z[0] = jnp.zeros(from_gx_z.shape[1:], F32)
+        from_gx_u[0] = jnp.zeros(from_gx_u.shape[1:], F32)
+
+    @pl.when(gx == n_gx - 1)
+    def _():
+        from_gx_z[1] = jnp.zeros(from_gx_z.shape[1:], F32)
+        from_gx_u[1] = jnp.zeros(from_gx_u.shape[1:], F32)
 
     def receive(stage):
-        for copy in copies[stage]:
-            copy.wait()
+        for b in range(bits):
+            gy_copy(stage, b).wait()
 
         @pl.when(gx > 0)
         def _():
@@ -338,7 +366,7 @@
                 blocks = [sources[span, i * LANES : (i + 1) * LANES] for i in range(own_blocks)]
                 near[f, span, cols] = lane_gather(blocks, lane, block_id)
     for f in range(FAR_DOT_FACES):
-        for at in range(0, cells, chunk_lanes):
+        for at in range(0, chunk_lanes, chunk_lanes):
             cols = slice(at, at + chunk_lanes)
             hot_part = one_hot(far[f : f + 1, cols], remote_pad)
             hot[f, 0:remote_pad, cols] = hot_part
@@ -432,7 +460,7 @@
     child_wide = jnp.broadcast_to(maps_all[2:3, :], (rows, hang_lanes))
     hang_zero = jnp.zeros((rows, hang_lanes), BF16)
 
-    fill_flat(source_flat, (source_ref,), width)
+    fill_flat(source_flat, source_ref, 0, width)
     for k in range(fields):
         own_hi, own_lo = split(sources[(fields + k) * rows : (fields + k + 1) * rows, :])
         z_hi[k, 0:rows, :] = own_hi
@@ -479,17 +507,30 @@
             z_hi[k, (1 + f) * rows : (2 + f) * rows, cols] = hi[span]
             z_lo[k, (1 + f) * rows : (2 + f) * rows, cols] = lo[span]
 
+    def gather_z(at, dot_faces):
+        cols = slice(at, at + chunk_lanes)
+        for f in range(dot_faces):
+            put_z(f, cols, near[f, width:, cols] + mm(far_both, hot[f, :, cols]))
+        for f in range(dot_faces, 6):
+            for first in range(at, at + chunk_lanes, LANES):
+                put_z(f, slice(first, first + LANES), far_gather(blocks_z, width, f, first))
+
+    def gather_u(at):
+        for f in range(6):
+            for first in range(at, at + chunk_lanes, LANES):
+                cols = slice(first, first + LANES)
+                hi, lo = split(far_gather(blocks_u, 0, f, first))
+                for k in range(fields):
+                    span = slice(k * rows, (k + 1) * rows)
+                    u_all[k, f, 0:rows, cols] = hi[span]
+                    u_all[k, f, rows : 2 * rows, cols] = lo[span]
+                    u_all[k, f, 2 * rows : 3 * rows, cols] = hi[span]
+
     receive(0)
     blocks_z = turn(from_gy_z, from_gx_z)
     halves = [split(block) for block in blocks_z]
     far_both = jnp.concatenate([h[0] for h in halves] + [h[1] for h in halves], 1)
-    for f in range(FAR_DOT_FACES):
-        for at in range(0, cells, chunk_lanes):
-            cols = slice(at, at + chunk_lanes)
-            put_z(f, cols, near[f, width:, cols] + mm(far_both, hot[f, :, cols]))
-    for f in range(FAR_DOT_FACES, 6):
-        for at in range(0, cells, LANES):
-            put_z(f, slice(at, at + LANES), far_gather(blocks_z, width, f, at))
+    gather_z(0, FAR_DOT_FACES)
 
     receive(1)
     blocks_u = turn(from_gy_u, from_gx_u)
@@ -502,43 +543,44 @@
         jnp.concatenate([jnp.where(face_wide == (f ^ 1), x, hang_zero) for f in range(6)], 0)
         for x in split(hang_all)
     ]
-    trace_parts = split(dot3(op_trace[:, 0 : 6 * rows], hang_hi, hang_lo))
-    trace_hi, trace_lo = [
-        jnp.concatenate([jnp.where(child_wide == h, x, hang_zero) for h in range(children)], 0)
-        for x in trace_parts
-    ]
-    lifted = dot3(op_back[...], trace_hi, trace_lo)
-    mains, ends = [], []
-    for k in range(fields):
-        at = k * hang_rows
-        block = lifted[:, at // LANES * LANES : at // LANES * LANES + LANES]
-        if at % LANES:
-            block = pltpu.roll(block, LANES - at % LANES, 1)
-        block = jnp.where(live_lanes, block, 0.0)
-        mains.append(block[0:tight])
-        ends.append(block[tight:rows])
-    lift_hi, lift_lo = split(jnp.concatenate(mains + ends, 0))
-    if 2 * hang_rows <= LANES:
-        lift_lo = pltpu.roll(lift_lo.astype(F32), hang_rows, 1)
-        lift = (lift_hi.astype(F32) + lift_lo).astype(BF16)[:, 0 : 2 * hang_rows]
-    else:
-        lift = jnp.concatenate([lift_hi[:, 0:hang_rows], lift_lo[:, 0:hang_rows]], 1)
+
+    def hang_traces():
+        trace_parts = split(dot3(op_trace[:, 0 : 6 * rows], hang_hi, hang_lo))
+        return [
+            jnp.concatenate([jnp.where(child_wide == h, x, hang_zero) for h in range(children)], 0)
+            for x in trace_parts
+        ]
+
+    def hang_lift(lifted):
+        mains, ends = [], []
+        for k in range(fields):
+            at = k * hang_rows
+            block = lifted[:, at // LANES * LANES : at // LANES * LANES + LANES]
+            if at % LANES:
+                block = pltpu.roll(block, LANES - at % LANES, 1)
+            block = jnp.where(live_lanes, block, 0.0)
+            mains.append(block[0:tight])
+            ends.append(block[tight:rows])
+        lift_hi, lift_lo = split(jnp.concatenate(mains + ends, 0))
+        if 2 * hang_rows <= LANES:
+            lift_lo = pltpu.roll(lift_lo.astype(F32), hang_rows, 1)
+            lift = (lift_hi.astype(F32) + lift_lo).astype(BF16)[:, 0 : 2 * hang_rows]
+        else:
+            lift = jnp.concatenate([lift_hi[:, 0:hang_rows], lift_lo[:, 0:hang_rows]], 1)
+        return lift
+
     end_rows = rows - tight
 
-    for f in range(6):
-        for at in range(0, cells, LANES):
-            cols = slice(at, at + LANES)
-            hi, lo = split(far_gather(blocks_u, 0, f, at))
-            for k in range(fields):
-                span = slice(k * rows, (k + 1) * rows)
-                u_all[k, f, 0:rows, cols] = hi[span]
-                u_all[k, f, rows : 2 * rows, cols] = lo[span]
-                u_all[k, f, 2 * rows : 3 * rows, cols] = hi[span]
     for at in range(0, cells, chunk_lanes):
         cols = slice(at, at + chunk_lanes)
         totals, end_totals = [], []
+        gather_u(at)
+        if at + chunk_lanes < cells:
+            gather_z(at + chunk_lanes, 0)
         for k in range(fields):
             forms = dot3(op_z[...], z_hi[k, :, cols], z_lo[k, :, cols])
+            if at == 0 and k == fields // 2:
+                traces = hang_traces()
             own_u = sources[k * rows : (k + 1) * rows, cols]
             src = jnp.concatenate(
                 [
@@ -560,23 +602,31 @@
             masks = [child == h for h in range(children)]
             sub = lax.broadcasted_iota(jnp.int32, (8, chunk_lanes), 0)
             end_mask = sub == child[0:8]
-            returned = mm(lift, scatter[f, :, cols])
             for k in range(fields):
                 jumps = mm(op_u[f, :, 0 : 3 * rows], u_all[k, f, :, cols])
                 jump = jumps[children * tight : 5 * tight]
                 for h in range(children):
                     jump = jnp.where(masks[h], jumps[h * tight : (h + 1) * tight], jump)
-                jump = jump + returned[k * tight : (k + 1) * tight]
                 totals[k] = totals[k] + jump * part_z[k, f * tight : (f + 1) * tight]
+                for e in range(tails):
+                    block = jumps[tail_at + 8 * e : tail_at + 8 * (e + 1)]
+                    block = jnp.where(end_mask, block, 0.0)
+                    weight = jnp.broadcast_to(part_x[k, 8 * e + f : 8 * e + f + 1, :], block.shape)
+                    end_totals[k] = end_totals[k] + block * weight
+            if at == 0 and f == 2:
+                lift = hang_lift(dot3(op_back[...], *traces))
+        for f in range(6):
+            returned = mm(lift, scatter[f, :, cols])
+            for k in range(fields):
+                back = returned[k * tight : (k + 1) * tight]
+                totals[k] = totals[k] + back * part_z[k, f * tight : (f + 1) * tight]
                 end_at = fields * tight + k * end_rows
                 for e in range(tails):
-                    block = jumps[tail_at + 8 * e : tail_at + 8 * (e + 1)]
-                    back = returned[end_at + 8 * (e // 8) : end_at + 8 * (e // 8) + 8]
+                    back = returned[end_at + e // 8 * 8 : end_at + e // 8 * 8 + 8]
                     if tails > 1:
                         back = jnp.where(sub == e % 8, back, 0.0)
-                    block = jnp.where(end_mask, block, 0.0) + back
-                    weight = jnp.broadcast_to(part_x[k, 8 * e + f : 8 * e + f + 1, :], block.shape)
-                    end_totals[k] = end_totals[k] + block * weight
+                    weight = jnp.broadcast_to(part_x[k, 8 * e + f : 8 * e + f + 1, :], back.shape)
+                    end_totals[k] = end_totals[k] + back * weight
         for k in range(fields):
             face_sum = jnp.sum(jnp.concatenate([totals[k], end_totals[k]], 0), axis=0, keepdims=True)
             row = fields + k
@@ -690,6 +740,7 @@
                 pltpu.SemaphoreType.DMA((2, bits)),
                 pltpu.SemaphoreType.DMA((2, 2)),
                 pltpu.SemaphoreType.DMA((2, 2)),
+                pltpu.SemaphoreType.REGULAR((bits + 1,)),
             ],
             compiler_params=pltpu.CompilerParams(collective_id=0, has_side_effects=True),
             name="indicators",

time: 12.5 us -> 11.9 us (0.952)
  Pallas kernels: 11 us -> 10.4 us
    pallas_call x1, Pallas kernels: 11 us -> 10.4 us  [shards(): pl.pallas_call(functools.partial(compute_kernel, dims, len(args)), out_sh...]
where the time goes in v3:
time: 11.9 us; the launch traced here: 11.7 us
  Pallas kernels  10.4 us (87%)
  between operations  0.65 us (5%)
  local copies, waits for them, and re-layouts  0.61 us (5%)
    pallas_call x1, Pallas kernels, shards(): pl.pallas_call(functools.partial(compute_kernel, dims, len(args)), out_sh...  10.4 us
    slice x1, local copies, waits for them, and re-layouts, shards(): return (raw[:fields], raw[fields:])  0.61 us

profile of v3, /device:TPU:0, one launch (start us, length us, event | category | flops | bytes accessed | tf_op | source)
XLA Modules:
  0.0 11.7 jit_solution(2851162042380164411)
XLA Ops:
  0.6 10.4 %indicators.1 = f32[8,512]{1,0:T(8,128)S(1)} custom-call(f32[27,4,512]{2,1,0:T(4,128)} %bitcast.9, f32[27,4,512]{2,1,0:T(4,128)} %bitcast.10, f32[27,4,512]{2,1,0:T(4,128)} %bitcast.11, f32[1,512]{1,0:T(1,128)} %bitcast.16, s32[1,512]{1,0:T(1,128)} %bitcast.17, f32[27,7,125]{2,1,0:T(8,128)} %bitcast.12, f32[27,125]{1,0:T(8,128)} %bitcast.14, ...), custom_call_target="tpu_custom_call" | custom-call | tf_op jit(solution)/shard_map/indicators/pallas_call | solution.py:694
  11.1 0.6 %fusion = (f32[4,512]{1,0:T(4,128)}, f32[4,512]{1,0:T(4,128)}) fusion(f32[8,512]{1,0:T(8,128)S(1)} %indicators.1), kind=kLoop, calls=%fused_computation | loop fusion | bytes 32768 | tf_op jit(solution)/shard_map/slice | solution.py:748

commit v4 on v3

--- a/solution.py
+++ b/solution.py
@@ -12,6 +12,7 @@
 F32 = jnp.float32
 BF16 = jnp.bfloat16
 MESH = pl.DeviceIdType.MESH
+EARLY_FORMS = 2
 DOT_FACES = 4
 FAR_DOT_FACES = 3
 
@@ -160,7 +161,8 @@
         pl.semaphore_signal(barrier, inc=1, device_id=(gx + 1, gy), device_id_type=MESH)
 
     order = [14, 15, 16, 1, 0, 11, 5, 6, 7, 8, 9, 10, 13, 12, 3, 4, 2]
-    loads = [pltpu.make_async_copy(hbm[i], local[i], in_sems.at[i]) for i in range(n_args)]
+    groups = [0 if i in order[:4] else 1 if i == order[4] else 2 for i in range(n_args)]
+    loads = [pltpu.make_async_copy(hbm[i], local[i], in_sems.at[groups[i]]) for i in range(n_args)]
     for i in order[:5]:
         loads[i].start()
 
@@ -172,6 +174,22 @@
         loads[i].wait()
     for i in order[5:]:
         loads[i].start()
+    lower = sum(bit_of) + jnp.minimum(gx, 1)
+
+    @pl.when(lower > 0)
+    def _():
+        pl.semaphore_wait(barrier, lower)
+
+    for b, partner in enumerate(partners):
+
+        @pl.when(bit_of[b] == 1)
+        def _():
+            pl.semaphore_signal(ready.at[b], inc=1, device_id=(gx, partner), device_id_type=MESH)
+
+    @pl.when(gx > 0)
+    def _():
+        pl.semaphore_signal(ready.at[bits], inc=1, device_id=(gx - 1, gy), device_id_type=MESH)
+
     for b, partner in enumerate(partners):
         ids[0:1, b * ghosts : (b + 1) * ghosts] = ghost_ref[0, pl.ds(partner, 1), :]
         at = main_pad + b * hangs
@@ -180,22 +198,6 @@
         at = bits * ghosts + side * edges
         ids[0:1, at : at + edges] = edge_ref[0, side : side + 1, :]
     chosen = jnp.maximum(ids[0:1, :], 0)
-
-    lower = sum(bit_of) + jnp.minimum(gx, 1)
-
-    @pl.when(lower > 0)
-    def _():
-        pl.semaphore_wait(barrier, lower)
-
-    for b, partner in enumerate(partners):
-
-        @pl.when(bit_of[b] == 1)
-        def _():
-            pl.semaphore_signal(ready.at[b], inc=1, device_id=(gx, partner), device_id_type=MESH)
-
-    @pl.when(gx > 0)
-    def _():
-        pl.semaphore_signal(ready.at[bits], inc=1, device_id=(gx - 1, gy), device_id_type=MESH)
 
     def pick(base, at):
         part = jnp.broadcast_to(chosen[:, at : at + LANES], (rows, LANES))
@@ -277,20 +279,6 @@
                 to_gy_u[b, ghosts : ghosts + hangs, :] = turned[at_slot : at_slot + hangs]
     send_lower(1)
 
-    for b in range(bits):
-
-        @pl.when(bit_of[b] == 0)
-        def _():
-            pl.semaphore_wait(ready.at[b], 1)
-            for stage in range(2):
-                gy_copy(stage, b).start()
-
-    @pl.when(gx < n_gx - 1)
-    def _():
-        pl.semaphore_wait(ready.at[bits], 1)
-        for stage in range(2):
-            high_copy(stage).start()
-
     @pl.when(gx == 0)
     def _():
         from_gx_z[0] = jnp.zeros(from_gx_z.shape[1:], F32)
@@ -336,7 +324,6 @@
             sources[group * rows : (group + 1) * rows, i * LANES : (i + 1) * LANES] = flat[
                 i, pl.ds(first, rows, stride=fields), :
             ]
-    own_both = both(sources[...])
     slot = slot_ref[...]
     shifted = slot - cells
     log_ghosts = ghosts.bit_length() - 1
@@ -350,21 +337,6 @@
         shifted < n_gy * ghosts, place_of * ghosts + within, shifted - (n_gy - bits) * ghosts
     )
     far = jnp.where(shifted < 0, -1, far)
-    for f in range(DOT_FACES):
-        for at in range(0, cells, chunk_lanes):
-            cols = slice(at, at + chunk_lanes)
-            got = mm(own_both, one_hot(slot[f : f + 1, cols], cells))
-            near[f, :, cols] = got[:wide] + got[wide:]
-    for f in range(DOT_FACES, 6):
-        for at in range(0, cells, LANES):
-            cols = slice(at, at + LANES)
-            part = jnp.broadcast_to(slot[f : f + 1, cols], (rows, LANES))
-            lane = jnp.bitwise_and(part, LANES - 1)
-            block_id = jnp.right_shift(part, 7)
-            for group in range(2 * fields):
-                span = slice(group * rows, (group + 1) * rows)
-                blocks = [sources[span, i * LANES : (i + 1) * LANES] for i in range(own_blocks)]
-                near[f, span, cols] = lane_gather(blocks, lane, block_id)
     for f in range(FAR_DOT_FACES):
         for at in range(0, chunk_lanes, chunk_lanes):
             cols = slice(at, at + chunk_lanes)
@@ -431,15 +403,6 @@
         partner = jnp.bitwise_xor(gy, 1 << b)
         for i in range(3):
             maps[i : i + 1, b * hangs : (b + 1) * hangs] = hang_ref[i, 0, pl.ds(partner, 1), :]
-    live = maps[0:1, :] >= 0
-    place = jnp.where(live, maps[0:1, :] + maps[1:2, :] * cells, -1).astype(F32)
-    place_rows = jnp.broadcast_to(place, (LANES, hang_pad)).T[0:hang_rows, 0:1]
-    column = lax.broadcasted_iota(jnp.int32, (hang_rows, cells), 1).astype(F32)
-    place_wide = jnp.broadcast_to(place_rows, (hang_rows, cells))
-    for f in range(6):
-        hit = jnp.where(place_wide == column + float(f * cells), 1.0, 0.0).astype(BF16)
-        scatter[f, 0:hang_rows] = hit
-        scatter[f, hang_rows : 2 * hang_rows] = hit
 
     def spread(x):
         outs = []
@@ -459,6 +422,13 @@
     face_wide = jnp.broadcast_to(maps_all[1:2, :], (rows, hang_lanes))
     child_wide = jnp.broadcast_to(maps_all[2:3, :], (rows, hang_lanes))
     hang_zero = jnp.zeros((rows, hang_lanes), BF16)
+    hang_cells = maps_all[0:1, :]
+    for first in range(0, hang_lanes, LANES):
+        cell_col = jnp.broadcast_to(hang_cells[:, first : first + LANES].astype(F32), (LANES, LANES)).T
+        for at in range(0, cells, LANES):
+            column = lax.broadcasted_iota(jnp.int32, (LANES, LANES), 1).astype(F32) + float(at)
+            hit = jnp.where(cell_col == column, 1.0, 0.0).astype(BF16)
+            scatter[first : first + LANES, at : at + LANES] = hit
 
     fill_flat(source_flat, source_ref, 0, width)
     for k in range(fields):
@@ -468,6 +438,36 @@
     coef = coef_ref[...]
     size = jnp.exp2(-levels_ref[...].astype(F32))
 
+    @pl.when(gx < n_gx - 1)
+    def _():
+        pl.semaphore_wait(ready.at[bits], 1)
+        for stage in range(2):
+            high_copy(stage).start()
+
+    for b in range(bits):
+
+        @pl.when(bit_of[b] == 0)
+        def _():
+            pl.semaphore_wait(ready.at[b], 1)
+            for stage in range(2):
+                gy_copy(stage, b).start()
+
+    own_both = both(sources[...])
+    for f in range(DOT_FACES):
+        for at in range(0, cells, chunk_lanes):
+            cols = slice(at, at + chunk_lanes)
+            got = mm(own_both, one_hot(slot[f : f + 1, cols], cells))
+            near[f, :, cols] = got[:wide] + got[wide:]
+    for f in range(DOT_FACES, 6):
+        for at in range(0, cells, LANES):
+            cols = slice(at, at + LANES)
+            part = jnp.broadcast_to(slot[f : f + 1, cols], (rows, LANES))
+            lane = jnp.bitwise_and(part, LANES - 1)
+            block_id = jnp.right_shift(part, 7)
+            for group in range(2 * fields):
+                span = slice(group * rows, (group + 1) * rows)
+                blocks = [sources[span, i * LANES : (i + 1) * LANES] for i in range(own_blocks)]
+                near[f, span, cols] = lane_gather(blocks, lane, block_id)
     far_lane = jnp.bitwise_and(far, LANES - 1)
     far_block = jnp.right_shift(far, 7)
 
@@ -526,18 +526,42 @@
                     u_all[k, f, rows : 2 * rows, cols] = lo[span]
                     u_all[k, f, 2 * rows : 3 * rows, cols] = hi[span]
 
+    totals = {at: [None] * fields for at in range(0, cells, chunk_lanes)}
+
+    def forms_of(k, at):
+        cols = slice(at, at + chunk_lanes)
+        forms = dot3(op_z[...], z_hi[k, :, cols], z_lo[k, :, cols])
+        own_u = sources[k * rows : (k + 1) * rows, cols]
+        src = jnp.concatenate(
+            [
+                source_flat[i, pl.ds(k, rows, stride=fields), :]
+                for i in range(at // LANES, (at + chunk_lanes) // LANES)
+            ],
+            1,
+        )
+        cell_part = src * forms[0:rows] - coef[:, cols] * own_u * forms[rows : 2 * rows]
+        cell_sum = jnp.sum(cell_part, axis=0, keepdims=True)
+        out_ref[k : k + 1, cols] = size[:, cols] * cell_sum * (1.0 / math.sqrt(quads))
+        part_z[k, :, cols] = forms[3 * rows : 3 * rows + 6 * tight]
+        part_x[k, 0 : 8 * tails, cols] = forms[3 * rows + 6 * tight : 3 * rows + 6 * tight + 8 * tails]
+        own_part = own_u * forms[2 * rows : 3 * rows]
+        totals[at][k] = sum(own_part[i : i + 8] for i in range(8, rows, 8)) + own_part[0:8]
+
     receive(0)
     blocks_z = turn(from_gy_z, from_gx_z)
     halves = [split(block) for block in blocks_z]
     far_both = jnp.concatenate([h[0] for h in halves] + [h[1] for h in halves], 1)
     gather_z(0, FAR_DOT_FACES)
+    for k in range(EARLY_FORMS):
+        forms_of(k, 0)
+    for at in range(chunk_lanes, cells, chunk_lanes):
+        gather_z(at, 0)
 
     receive(1)
     blocks_u = turn(from_gy_u, from_gx_u)
     parts = [from_gy_u[b, ghosts : ghosts + hangs, :] for b in range(bits)]
     parts.append(jnp.zeros((hang_pad - hang_count, width), F32))
     hang_flat[...] = jnp.concatenate(parts, 0).T
-    live_lanes = lax.broadcasted_iota(jnp.int32, (rows, LANES), 1) < hang_rows
     hang_all = spread([hang_flat[pl.ds(k, rows, stride=fields), :] for k in range(fields)])
     hang_hi, hang_lo = [
         jnp.concatenate([jnp.where(face_wide == (f ^ 1), x, hang_zero) for f in range(6)], 0)
@@ -551,84 +575,90 @@
             for x in trace_parts
         ]
 
-    def hang_lift(lifted):
-        mains, ends = [], []
+    def hang_terms(lifted):
+        sub = lax.broadcasted_iota(jnp.int32, (8, LANES), 0)
+        outs = []
+        for first in range(0, hang_lanes, LANES):
+            span = slice(first, first + LANES)
+            safe = jnp.maximum(hang_cells[:, span], 0)
+            face = maps_all[1:2, span]
+            field = (lax.broadcasted_iota(jnp.int32, (1, LANES), 1) + first) // hang_rows
+            live_fields = [k for k in range(fields) if first <= k * hang_rows < first + LANES]
+
+            def weights(ref, count):
+                lane = jnp.broadcast_to(jnp.bitwise_and(safe, LANES - 1), (count, LANES))
+                block_id = jnp.broadcast_to(jnp.right_shift(safe, 7), (count, LANES))
+                total = jnp.zeros((count, LANES), F32)
+                for k in live_fields:
+                    blocks = [ref[k, 0:count, i * LANES : (i + 1) * LANES] for i in range(own_blocks)]
+                    mine = jnp.broadcast_to(field == k, (count, LANES))
+                    total = jnp.where(mine, lane_gather(blocks, lane, block_id), total)
+                return total
+
+            main_weights = weights(part_z, 6 * tight)
+            chosen_weights = jnp.zeros((tight, LANES), F32)
+            for f in range(6):
+                mine = jnp.broadcast_to(face == f, (tight, LANES))
+                chosen_weights = jnp.where(
+                    mine, main_weights[f * tight : (f + 1) * tight], chosen_weights
+                )
+            product = chosen_weights * lifted[0:tight, span]
+            total = sum(product[i : i + 8] for i in range(0, tight, 8))
+            if tails:
+                end_weights = weights(part_x, 8 * tails)
+                mine = sub == jnp.broadcast_to(face, (8, LANES))
+                for e in range(tails):
+                    row = jnp.broadcast_to(lifted[tight + e : tight + e + 1, span], (8, LANES))
+                    picked = jnp.where(mine, end_weights[8 * e : 8 * (e + 1)], 0.0)
+                    total = total + picked * row
+            total = jnp.broadcast_to(jnp.sum(total, axis=0, keepdims=True), (8, LANES))
+            outs.append(jnp.where(sub == jnp.broadcast_to(field, (8, LANES)), total, 0.0))
+        return both(outs[0] if len(outs) == 1 else jnp.concatenate(outs, 1))
+
+
+    def face_terms(f, at):
+        cols = slice(at, at + chunk_lanes)
+        child = jnp.broadcast_to(child_ref[f : f + 1, cols], (tight, chunk_lanes))
+        masks = [child == h for h in range(children)]
+        end_mask = lax.broadcasted_iota(jnp.int32, (8, chunk_lanes), 0) == child[0:8]
         for k in range(fields):
-            at = k * hang_rows
-            block = lifted[:, at // LANES * LANES : at // LANES * LANES + LANES]
-            if at % LANES:
-                block = pltpu.roll(block, LANES - at % LANES, 1)
-            block = jnp.where(live_lanes, block, 0.0)
-            mains.append(block[0:tight])
-            ends.append(block[tight:rows])
-        lift_hi, lift_lo = split(jnp.concatenate(mains + ends, 0))
-        if 2 * hang_rows <= LANES:
-            lift_lo = pltpu.roll(lift_lo.astype(F32), hang_rows, 1)
-            lift = (lift_hi.astype(F32) + lift_lo).astype(BF16)[:, 0 : 2 * hang_rows]
-        else:
-            lift = jnp.concatenate([lift_hi[:, 0:hang_rows], lift_lo[:, 0:hang_rows]], 1)
-        return lift
-
-    end_rows = rows - tight
-
-    for at in range(0, cells, chunk_lanes):
+            jumps = mm(op_u[f, :, 0 : 3 * rows], u_all[k, f, :, cols])
+            jump = jumps[children * tight : 5 * tight]
+            for h in range(children):
+                jump = jnp.where(masks[h], jumps[h * tight : (h + 1) * tight], jump)
+            product = jump * part_z[k, f * tight : (f + 1) * tight, cols]
+            for i in range(0, tight, 8):
+                totals[at][k] = totals[at][k] + product[i : i + 8]
+            for e in range(tails):
+                block = jumps[tail_at + 8 * e : tail_at + 8 * (e + 1)]
+                block = jnp.where(end_mask, block, 0.0)
+                row = 8 * e + f
+                weight = jnp.broadcast_to(part_x[k, row : row + 1, cols], block.shape)
+                totals[at][k] = totals[at][k] + block * weight
+
+    chunks = list(range(0, cells, chunk_lanes))
+    for k in range(EARLY_FORMS, fields):
+        forms_of(k, 0)
+    for n, at in enumerate(chunks):
+        gather_u(at)
+        if n > 0:
+            for k in range(fields):
+                forms_of(k, at)
+                if n == 1 and k == 1:
+                    traces = hang_traces()
+        if n == 1:
+            lifted = dot3(op_back[...], *traces)
+    terms = hang_terms(lifted)
+    for at in chunks:
+        for f in range(6):
+            face_terms(f, at)
+            if at == chunks[-1] and f == 2:
+                back = mm(terms, scatter[...])
+                returned = back[0:8] + back[8:16]
+    for at in chunks:
         cols = slice(at, at + chunk_lanes)
-        totals, end_totals = [], []
-        gather_u(at)
-        if at + chunk_lanes < cells:
-            gather_z(at + chunk_lanes, 0)
         for k in range(fields):
-            forms = dot3(op_z[...], z_hi[k, :, cols], z_lo[k, :, cols])
-            if at == 0 and k == fields // 2:
-                traces = hang_traces()
-            own_u = sources[k * rows : (k + 1) * rows, cols]
-            src = jnp.concatenate(
-                [
-                    source_flat[i, pl.ds(k, rows, stride=fields), :]
-                    for i in range(at // LANES, (at + chunk_lanes) // LANES)
-                ],
-                1,
-            )
-            cell_part = src * forms[0:rows] - coef[:, cols] * own_u * forms[rows : 2 * rows]
-            cell_sum = jnp.sum(cell_part, axis=0, keepdims=True)
-            out_ref[k : k + 1, cols] = size[:, cols] * cell_sum * (1.0 / math.sqrt(quads))
-            part_z[k] = forms[3 * rows : 3 * rows + 6 * tight]
-            part_x[k] = forms[3 * rows + 6 * tight : 3 * rows + 6 * tight + 8 * tails]
-            own_part = own_u * forms[2 * rows : 3 * rows]
-            end_totals.append(sum(own_part[i : i + 8] for i in range(8, rows, 8)) + own_part[0:8])
-            totals.append(jnp.zeros((tight, chunk_lanes), F32))
-        for f in range(6):
-            child = jnp.broadcast_to(child_ref[f : f + 1, cols], (tight, chunk_lanes))
-            masks = [child == h for h in range(children)]
-            sub = lax.broadcasted_iota(jnp.int32, (8, chunk_lanes), 0)
-            end_mask = sub == child[0:8]
-            for k in range(fields):
-                jumps = mm(op_u[f, :, 0 : 3 * rows], u_all[k, f, :, cols])
-                jump = jumps[children * tight : 5 * tight]
-                for h in range(children):
-                    jump = jnp.where(masks[h], jumps[h * tight : (h + 1) * tight], jump)
-                totals[k] = totals[k] + jump * part_z[k, f * tight : (f + 1) * tight]
-                for e in range(tails):
-                    block = jumps[tail_at + 8 * e : tail_at + 8 * (e + 1)]
-                    block = jnp.where(end_mask, block, 0.0)
-                    weight = jnp.broadcast_to(part_x[k, 8 * e + f : 8 * e + f + 1, :], block.shape)
-                    end_totals[k] = end_totals[k] + block * weight
-            if at == 0 and f == 2:
-                lift = hang_lift(dot3(op_back[...], *traces))
-        for f in range(6):
-            returned = mm(lift, scatter[f, :, cols])
-            for k in range(fields):
-                back = returned[k * tight : (k + 1) * tight]
-                totals[k] = totals[k] + back * part_z[k, f * tight : (f + 1) * tight]
-                end_at = fields * tight + k * end_rows
-                for e in range(tails):
-                    back = returned[end_at + e // 8 * 8 : end_at + e // 8 * 8 + 8]
-                    if tails > 1:
-                        back = jnp.where(sub == e % 8, back, 0.0)
-                    weight = jnp.broadcast_to(part_x[k, 8 * e + f : 8 * e + f + 1, :], back.shape)
-                    end_totals[k] = end_totals[k] + back * weight
-        for k in range(fields):
-            face_sum = jnp.sum(jnp.concatenate([totals[k], end_totals[k]], 0), axis=0, keepdims=True)
+            face_sum = jnp.sum(totals[at][k], axis=0, keepdims=True) + returned[k : k + 1, cols]
             row = fields + k
             out_ref[row : row + 1, cols] = size[:, cols] * face_sum * (1.0 / math.sqrt(6 * points))
 
@@ -721,9 +751,9 @@
                 pltpu.VMEM((fields * rows, hang_pad), F32),
                 pltpu.VMEM((6, wide, cells), F32),
                 pltpu.VMEM((6, 2 * main_pad, cells), BF16),
-                pltpu.VMEM((6, 2 * hang_rows, cells), BF16),
-                pltpu.VMEM((fields, 6 * tight, chunk), F32),
-                pltpu.VMEM((fields, max(8 * tails, 8), chunk), F32),
+                pltpu.VMEM((fields * hang_rows, cells), BF16),
+                pltpu.VMEM((fields, 6 * tight, cells), F32),
+                pltpu.VMEM((fields, max(8 * tails, 8), cells), F32),
             ]
             + [
                 pltpu.VMEM((bits, ghosts + hangs, wide // 2), F32),
@@ -735,7 +765,7 @@
             + [
                 pltpu.VMEM((8, main_pad + hang_pad), jnp.int32),
                 pltpu.VMEM((wide, LANES), F32),
-                pltpu.SemaphoreType.DMA((len(args),)),
+                pltpu.SemaphoreType.DMA((3,)),
                 pltpu.SemaphoreType.DMA((2, bits)),
                 pltpu.SemaphoreType.DMA((2, bits)),
                 pltpu.SemaphoreType.DMA((2, 2)),

time: 11.9 us -> 11.3 us (0.950)
  Pallas kernels: 10.4 us -> 9.88 us
    pallas_call x1, Pallas kernels: 10.4 us -> 9.88 us  [shards(): pl.pallas_call(functools.partial(compute_kernel, dims, len(args)), out_sh...]
where the time goes in v4:
time: 11.3 us; the launch traced here: 11.1 us
  Pallas kernels  9.88 us (87%)
  between operations  0.65 us (6%)
  local copies, waits for them, and re-layouts  0.61 us (5%)
    pallas_call x1, Pallas kernels, shards(): pl.pallas_call(functools.partial(compute_kernel, dims, len(args)), out_sh...  9.88 us
    slice x1, local copies, waits for them, and re-layouts, shards(): return (raw[:fields], raw[fields:])  0.61 us

profile of v4, /device:TPU:0, one launch (start us, length us, event | category | flops | bytes accessed | tf_op | source)
XLA Modules:
  0.0 11.1 jit_solution(6733688800829210872)
XLA Ops:
  0.6 9.9 %indicators.1 = f32[8,512]{1,0:T(8,128)S(1)} custom-call(f32[27,4,512]{2,1,0:T(4,128)} %bitcast.9, f32[27,4,512]{2,1,0:T(4,128)} %bitcast.10, f32[27,4,512]{2,1,0:T(4,128)} %bitcast.11, f32[1,512]{1,0:T(1,128)} %bitcast.16, s32[1,512]{1,0:T(1,128)} %bitcast.17, f32[27,7,125]{2,1,0:T(8,128)} %bitcast.12, f32[27,125]{1,0:T(8,128)} %bitcast.14, ...), custom_call_target="tpu_custom_call" | custom-call | tf_op jit(solution)/shard_map/indicators/pallas_call | solution.py:724
  10.5 0.6 %fusion = (f32[4,512]{1,0:T(4,128)}, f32[4,512]{1,0:T(4,128)}) fusion(f32[8,512]{1,0:T(8,128)S(1)} %indicators.1), kind=kLoop, calls=%fused_computation | loop fusion | bytes 32768 | tf_op jit(solution)/shard_map/slice | solution.py:778

commit v5 on v4

--- a/solution.py
+++ b/solution.py
@@ -88,13 +88,14 @@
         child_flat,
         op_flux,
         op_rep,
-        op_z,
+        op_near,
+        op_own,
         op_u,
         op_trace,
         op_back,
         maps,
-        z_hi,
-        z_lo,
+        z_near,
+        own_forms,
         u_all,
         sources,
         flat,
@@ -116,10 +117,8 @@
         ids,
         packed,
         in_sems,
-        send_gy,
-        recv_gy,
-        send_gx,
-        recv_gx,
+        send_sems,
+        recv_sems,
         ready,
     ) = refs[2 * n_args + 1 :]
     (
@@ -226,8 +225,8 @@
         return pltpu.make_async_remote_copy(
             src_ref=src.at[b],
             dst_ref=dst.at[b],
-            send_sem=send_gy.at[stage, b],
-            recv_sem=recv_gy.at[stage, b],
+            send_sem=send_sems.at[stage, 0],
+            recv_sem=recv_sems.at[stage, 0],
             device_id=(gx, partners[b]),
             device_id_type=MESH,
         )
@@ -237,8 +236,8 @@
         return pltpu.make_async_remote_copy(
             src_ref=src.at[0],
             dst_ref=dst.at[1],
-            send_sem=send_gx.at[stage, 0],
-            recv_sem=recv_gx.at[stage, 1],
+            send_sem=send_sems.at[stage, 1],
+            recv_sem=recv_sems.at[stage, 1],
             device_id=(gx - 1, gy),
             device_id_type=MESH,
         )
@@ -248,8 +247,8 @@
         return pltpu.make_async_remote_copy(
             src_ref=src.at[1],
             dst_ref=dst.at[0],
-            send_sem=send_gx.at[stage, 1],
-            recv_sem=recv_gx.at[stage, 0],
+            send_sem=send_sems.at[stage, 1],
+            recv_sem=recv_sems.at[stage, 1],
             device_id=(gx + 1, gy),
             device_id_type=MESH,
         )
@@ -289,19 +288,25 @@
         from_gx_z[1] = jnp.zeros(from_gx_z.shape[1:], F32)
         from_gx_u[1] = jnp.zeros(from_gx_u.shape[1:], F32)
 
+    def wait_all(gy_ref, gx_ref, sems):
+        def wait(ref, sem):
+            pltpu.make_async_copy(ref, ref, sem).wait()
+
+        wait(gy_ref, sems.at[0])
+
+        @pl.when((gx > 0) & (gx < n_gx - 1))
+        def _():
+            wait(gx_ref, sems.at[1])
+
+        if n_gx > 1:
+
+            @pl.when((gx == 0) | (gx == n_gx - 1))
+            def _():
+                wait(gx_ref.at[0], sems.at[1])
+
     def receive(stage):
-        for b in range(bits):
-            gy_copy(stage, b).wait()
-
-        @pl.when(gx > 0)
-        def _():
-            low_copy(stage).wait_send()
-            high_copy(stage).wait_recv()
-
-        @pl.when(gx < n_gx - 1)
-        def _():
-            high_copy(stage).wait_send()
-            low_copy(stage).wait_recv()
+        _, dst, _, far_gx = stages[stage]
+        wait_all(dst, far_gx, recv_sems.at[stage])
 
     quads = recon_ref.shape[2]
     own_blocks = cells // LANES
@@ -312,7 +317,10 @@
     children = 4
     tight = points // 8 * 8
     tails = points - tight
-    form_rows = op_z.shape[0] // 2
+    dof_tight = dofs // 8 * 8
+    form_rows = op_own.shape[0]
+    pack_rows = 6 * dof_tight + 24
+    cut_row = 256 - pack_rows - pack_rows % 16
     tail_at = 5 * tight
 
     for i in order[5:]:
@@ -338,11 +346,19 @@
     )
     far = jnp.where(shifted < 0, -1, far)
     for f in range(FAR_DOT_FACES):
-        for at in range(0, chunk_lanes, chunk_lanes):
+        for at in range(0, cells, chunk_lanes):
             cols = slice(at, at + chunk_lanes)
             hot_part = one_hot(far[f : f + 1, cols], remote_pad)
             hot[f, 0:remote_pad, cols] = hot_part
             hot[f, remote_pad : 2 * remote_pad, cols] = hot_part
+
+    def pack_near(piece):
+        mains = [piece(f)[0:dof_tight] for f in range(6)]
+        ends = [
+            piece(f)[dof_tight:rows] + pltpu.roll(piece(f + 1)[dof_tight:rows], 4, 0)
+            for f in range(0, 6, 2)
+        ]
+        return jnp.concatenate(mains + ends, 0)
 
     op_recon[...] = jnp.zeros_like(op_recon)
     op_left[...] = jnp.zeros_like(op_left)
@@ -370,8 +386,24 @@
         op_child[h * rows : (h + 1) * rows, :] = child_flat[pl.ds(h, rows, stride=children), :]
     flux_turned = op_flux_rows[...].T[0:rows]
     op_left[2 * rows : 3 * rows, :] = dot3(both(flux_turned), *split(op_face_rows[...]))
-    recon_turned = jnp.concatenate([op_recon[pl.ds(f, rows, stride=8), :] for f in range(7)], 0)
-    op_z[...] = both(dot3(both(op_left[...]), *split(recon_turned), dot=mm_nt))
+    turned = [op_recon[pl.ds(f, rows, stride=8), :] for f in range(7)]
+    order_near = pack_near(lambda f: turned[1 + f])
+    spare = jnp.zeros((256 - pack_rows - cut_row, op_recon.shape[1]), F32)
+    order_all = jnp.concatenate(
+        [order_near, order_near[0:cut_row], spare, order_near, order_near[cut_row:]]
+        + [turned[0]] * 3
+        + [jnp.zeros((LANES - 3 * rows, op_recon.shape[1]), F32)],
+        0,
+    )
+    ops_hi, ops_lo = split(dot3(both(op_left[...]), *split(order_all), dot=mm_nt))
+    op_near[0] = ops_hi[:, 0:256]
+    lane_of = lax.broadcasted_iota(jnp.int32, (form_rows, 256), 1)
+    mixed = jnp.where(lane_of < pack_rows, ops_lo[:, 256:512].astype(F32), ops_hi[:, 256:512].astype(F32))
+    op_near[1] = mixed.astype(BF16)
+    mixed = jnp.where(
+        lane_of[:, 0:LANES] < 2 * rows, ops_hi[:, 512:].astype(F32), ops_lo[:, 512:].astype(F32)
+    )
+    op_own[...] = mixed.astype(BF16)
     for f in range(6):
         single = op_flux_rows[f * rows : (f + 1) * rows, :]
         thrice = single + pltpu.roll(single, rows, 1) + pltpu.roll(single, 2 * rows, 1)
@@ -431,10 +463,6 @@
             scatter[first : first + LANES, at : at + LANES] = hit
 
     fill_flat(source_flat, source_ref, 0, width)
-    for k in range(fields):
-        own_hi, own_lo = split(sources[(fields + k) * rows : (fields + k + 1) * rows, :])
-        z_hi[k, 0:rows, :] = own_hi
-        z_lo[k, 0:rows, :] = own_lo
     coef = coef_ref[...]
     size = jnp.exp2(-levels_ref[...].astype(F32))
 
@@ -468,6 +496,12 @@
                 span = slice(group * rows, (group + 1) * rows)
                 blocks = [sources[span, i * LANES : (i + 1) * LANES] for i in range(own_blocks)]
                 near[f, span, cols] = lane_gather(blocks, lane, block_id)
+    for k in range(fields):
+        own_hi, own_lo = split(sources[(fields + k) * rows : (fields + k + 1) * rows, :])
+        for at in range(0, cells, chunk_lanes):
+            cols = slice(at, at + chunk_lanes)
+            thrice = jnp.concatenate([own_hi[:, cols], own_lo[:, cols], own_hi[:, cols]], 0)
+            own_forms[k, :, cols] = mm(op_own[:, 0 : 3 * rows], thrice)
     far_lane = jnp.bitwise_and(far, LANES - 1)
     far_block = jnp.right_shift(far, 7)
 
@@ -501,11 +535,8 @@
         return jnp.concatenate(outs, 0)
 
     def put_z(f, cols, total):
-        hi, lo = split(total)
         for k in range(fields):
-            span = slice(k * rows, (k + 1) * rows)
-            z_hi[k, (1 + f) * rows : (2 + f) * rows, cols] = hi[span]
-            z_lo[k, (1 + f) * rows : (2 + f) * rows, cols] = lo[span]
+            z_near[k, f * rows : (f + 1) * rows, cols] = total[k * rows : (k + 1) * rows]
 
     def gather_z(at, dot_faces):
         cols = slice(at, at + chunk_lanes)
@@ -524,18 +555,25 @@
                     span = slice(k * rows, (k + 1) * rows)
                     u_all[k, f, 0:rows, cols] = hi[span]
                     u_all[k, f, rows : 2 * rows, cols] = lo[span]
-                    u_all[k, f, 2 * rows : 3 * rows, cols] = hi[span]
 
     totals = {at: [None] * fields for at in range(0, cells, chunk_lanes)}
 
+    form_lanes = cells
+
     def forms_of(k, at):
-        cols = slice(at, at + chunk_lanes)
-        forms = dot3(op_z[...], z_hi[k, :, cols], z_lo[k, :, cols])
+        cols = slice(at, at + form_lanes)
+        packed_z = pack_near(lambda f: z_near[k, f * rows : (f + 1) * rows, cols])
+        high = packed_z.astype(BF16).astype(F32)
+        low = packed_z - high
+        fill = jnp.zeros((256 - pack_rows - cut_row, form_lanes), F32)
+        first = jnp.concatenate([high, low[0:cut_row], fill], 0).astype(BF16)
+        second = jnp.concatenate([high, low[cut_row:]], 0).astype(BF16)
+        forms = mm(op_near[0], first) + mm(op_near[1], second) + own_forms[k, :, cols]
         own_u = sources[k * rows : (k + 1) * rows, cols]
         src = jnp.concatenate(
             [
                 source_flat[i, pl.ds(k, rows, stride=fields), :]
-                for i in range(at // LANES, (at + chunk_lanes) // LANES)
+                for i in range(at // LANES, (at + form_lanes) // LANES)
             ],
             1,
         )
@@ -545,17 +583,20 @@
         part_z[k, :, cols] = forms[3 * rows : 3 * rows + 6 * tight]
         part_x[k, 0 : 8 * tails, cols] = forms[3 * rows + 6 * tight : 3 * rows + 6 * tight + 8 * tails]
         own_part = own_u * forms[2 * rows : 3 * rows]
-        totals[at][k] = sum(own_part[i : i + 8] for i in range(8, rows, 8)) + own_part[0:8]
-
+        own_sum = sum(own_part[i : i + 8] for i in range(8, rows, 8)) + own_part[0:8]
+        for first in range(at, at + form_lanes, chunk_lanes):
+            totals[first][k] = own_sum[:, first - at : first - at + chunk_lanes]
+
+    for stage in range(2):
+        wait_all(stages[stage][0], stages[stage][2], send_sems.at[stage])
     receive(0)
     blocks_z = turn(from_gy_z, from_gx_z)
     halves = [split(block) for block in blocks_z]
     far_both = jnp.concatenate([h[0] for h in halves] + [h[1] for h in halves], 1)
-    gather_z(0, FAR_DOT_FACES)
+    for at in range(0, cells, chunk_lanes):
+        gather_z(at, FAR_DOT_FACES)
     for k in range(EARLY_FORMS):
         forms_of(k, 0)
-    for at in range(chunk_lanes, cells, chunk_lanes):
-        gather_z(at, 0)
 
     receive(1)
     blocks_u = turn(from_gy_u, from_gx_u)
@@ -622,7 +663,8 @@
         masks = [child == h for h in range(children)]
         end_mask = lax.broadcasted_iota(jnp.int32, (8, chunk_lanes), 0) == child[0:8]
         for k in range(fields):
-            jumps = mm(op_u[f, :, 0 : 3 * rows], u_all[k, f, :, cols])
+            pair = u_all[k, f, :, cols]
+            jumps = mm(op_u[f, :, 0 : 3 * rows], jnp.concatenate([pair, pair[0:rows]], 0))
             jump = jumps[children * tight : 5 * tight]
             for h in range(children):
                 jump = jnp.where(masks[h], jumps[h * tight : (h + 1) * tight], jump)
@@ -639,15 +681,12 @@
     chunks = list(range(0, cells, chunk_lanes))
     for k in range(EARLY_FORMS, fields):
         forms_of(k, 0)
-    for n, at in enumerate(chunks):
+        if k == max(EARLY_FORMS, fields - 3):
+            traces = hang_traces()
+        if k == fields - 1:
+            lifted = dot3(op_back[...], *traces)
+    for at in chunks:
         gather_u(at)
-        if n > 0:
-            for k in range(fields):
-                forms_of(k, at)
-                if n == 1 and k == 1:
-                    traces = hang_traces()
-        if n == 1:
-            lifted = dot3(op_back[...], *traces)
     terms = hang_terms(lifted)
     for at in chunks:
         for f in range(6):
@@ -737,14 +776,15 @@
                 pltpu.VMEM((4 * rows, LANES), F32),
                 pltpu.VMEM((rows, round_up(6 * rows, LANES)), F32),
                 pltpu.VMEM((rows, 6 * LANES), F32),
-                pltpu.VMEM((2 * form_rows, 7 * rows), BF16),
+                pltpu.VMEM((2, form_rows, 256), BF16),
+                pltpu.VMEM((form_rows, LANES), BF16),
                 pltpu.VMEM((6, map_rows, LANES), BF16),
                 pltpu.VMEM((2 * rows, round_up(6 * rows, LANES)), BF16),
                 pltpu.VMEM((2 * rows, 4 * rows), BF16),
                 pltpu.VMEM((8, hang_pad), jnp.int32),
-                pltpu.VMEM((fields, 7 * rows, cells), BF16),
-                pltpu.VMEM((fields, 7 * rows, cells), BF16),
-                pltpu.VMEM((fields, 6, 3 * rows, cells), BF16),
+                pltpu.VMEM((fields, 6 * rows, cells), F32),
+                pltpu.VMEM((fields, form_rows, cells), F32),
+                pltpu.VMEM((fields, 6, 2 * rows, cells), BF16),
                 pltpu.VMEM((wide, cells), F32),
                 pltpu.VMEM((max(cells, main_pad) // LANES, wide, LANES), F32),
                 pltpu.VMEM((cells // LANES, fields * rows, LANES), F32),
@@ -766,8 +806,6 @@
                 pltpu.VMEM((8, main_pad + hang_pad), jnp.int32),
                 pltpu.VMEM((wide, LANES), F32),
                 pltpu.SemaphoreType.DMA((3,)),
-                pltpu.SemaphoreType.DMA((2, bits)),
-                pltpu.SemaphoreType.DMA((2, bits)),
                 pltpu.SemaphoreType.DMA((2, 2)),
                 pltpu.SemaphoreType.DMA((2, 2)),
                 pltpu.SemaphoreType.REGULAR((bits + 1,)),

time: 11.3 us -> 11 us (0.973)
  Pallas kernels: 9.88 us -> 9.62 us
    pallas_call x1, Pallas kernels: 9.88 us -> 9.62 us  [shards(): pl.pallas_call(functools.partial(compute_kernel, dims, len(args)), out_sh...]
where the time goes in v5:
time: 11 us; the launch traced here: 10.9 us
  Pallas kernels  9.62 us (87%)
  between operations  0.65 us (6%)
  local copies, waits for them, and re-layouts  0.61 us (6%)
    pallas_call x1, Pallas kernels, shards(): pl.pallas_call(functools.partial(compute_kernel, dims, len(args)), out_sh...  9.62 us
    slice x1, local copies, waits for them, and re-layouts, shards(): return (raw[:fields], raw[fields:])  0.61 us

profile of v5, /device:TPU:0, one launch (start us, length us, event | category | flops | bytes accessed | tf_op | source)
XLA Modules:
  0.0 10.9 jit_solution(7738186114524285853)
XLA Ops:
  0.6 9.6 %indicators.1 = f32[8,512]{1,0:T(8,128)S(1)} custom-call(f32[27,4,512]{2,1,0:T(4,128)} %bitcast.9, f32[27,4,512]{2,1,0:T(4,128)} %bitcast.10, f32[27,4,512]{2,1,0:T(4,128)} %bitcast.11, f32[1,512]{1,0:T(1,128)} %bitcast.16, s32[1,512]{1,0:T(1,128)} %bitcast.17, f32[27,7,125]{2,1,0:T(8,128)} %bitcast.12, f32[27,125]{1,0:T(8,128)} %bitcast.14, ...), custom_call_target="tpu_custom_call" | custom-call | tf_op jit(solution)/shard_map/indicators/pallas_call | solution.py:763
  10.3 0.6 %fusion = (f32[4,512]{1,0:T(4,128)}, f32[4,512]{1,0:T(4,128)}) fusion(f32[8,512]{1,0:T(8,128)S(1)} %indicators.1), kind=kLoop, calls=%fused_computation | loop fusion | bytes 32768 | tf_op jit(solution)/shard_map/slice | solution.py:816

commit v6 on v5

--- a/solution.py
+++ b/solution.py
@@ -171,24 +171,6 @@
     ids[...] = jnp.zeros_like(ids)
     for i in order[:4]:
         loads[i].wait()
-    for i in order[5:]:
-        loads[i].start()
-    lower = sum(bit_of) + jnp.minimum(gx, 1)
-
-    @pl.when(lower > 0)
-    def _():
-        pl.semaphore_wait(barrier, lower)
-
-    for b, partner in enumerate(partners):
-
-        @pl.when(bit_of[b] == 1)
-        def _():
-            pl.semaphore_signal(ready.at[b], inc=1, device_id=(gx, partner), device_id_type=MESH)
-
-    @pl.when(gx > 0)
-    def _():
-        pl.semaphore_signal(ready.at[bits], inc=1, device_id=(gx - 1, gy), device_id_type=MESH)
-
     for b, partner in enumerate(partners):
         ids[0:1, b * ghosts : (b + 1) * ghosts] = ghost_ref[0, pl.ds(partner, 1), :]
         at = main_pad + b * hangs
@@ -266,7 +248,25 @@
 
     fill_flat(flat, adjoint_ref, width, width)
     pack(width, to_gy_z, to_gx_z)
+    lower = sum(bit_of) + jnp.minimum(gx, 1)
+
+    @pl.when(lower > 0)
+    def _():
+        pl.semaphore_wait(barrier, lower)
+
     send_lower(0)
+    for b, partner in enumerate(partners):
+
+        @pl.when(bit_of[b] == 1)
+        def _():
+            pl.semaphore_signal(ready.at[b], inc=1, device_id=(gx, partner), device_id_type=MESH)
+
+    @pl.when(gx > 0)
+    def _():
+        pl.semaphore_signal(ready.at[bits], inc=1, device_id=(gx - 1, gy), device_id_type=MESH)
+
+    for i in order[5:]:
+        loads[i].start()
     loads[order[4]].wait()
     fill_flat(flat, primal_ref, 0, width)
     pack(0, to_gy_u, to_gx_u)
@@ -687,11 +687,12 @@
             lifted = dot3(op_back[...], *traces)
     for at in chunks:
         gather_u(at)
-    terms = hang_terms(lifted)
     for at in chunks:
         for f in range(6):
             face_terms(f, at)
-            if at == chunks[-1] and f == 2:
+            if at == chunks[0] and f == 3:
+                terms = hang_terms(lifted)
+            if at == chunks[-1] and f == 4:
                 back = mm(terms, scatter[...])
                 returned = back[0:8] + back[8:16]
     for at in chunks:

time: 11 us -> 11 us (level)
  no operation moved by 1% of the time
where the time goes in v6:
time: 11 us; the launch traced here: 10.8 us
  Pallas kernels  9.58 us (87%)
  between operations  0.65 us (6%)
  local copies, waits for them, and re-layouts  0.61 us (6%)
    pallas_call x1, Pallas kernels, shards(): pl.pallas_call(functools.partial(compute_kernel, dims, len(args)), out_sh...  9.58 us
    slice x1, local copies, waits for them, and re-layouts, shards(): return (raw[:fields], raw[fields:])  0.61 us

profile of v6, /device:TPU:0, one launch (start us, length us, event | category | flops | bytes accessed | tf_op | source)
XLA Modules:
  0.0 10.8 jit_solution(12009163496936489295)
XLA Ops:
  0.6 9.6 %indicators.1 = f32[8,512]{1,0:T(8,128)S(1)} custom-call(f32[27,4,512]{2,1,0:T(4,128)} %bitcast.9, f32[27,4,512]{2,1,0:T(4,128)} %bitcast.10, f32[27,4,512]{2,1,0:T(4,128)} %bitcast.11, f32[1,512]{1,0:T(1,128)} %bitcast.16, s32[1,512]{1,0:T(1,128)} %bitcast.17, f32[27,7,125]{2,1,0:T(8,128)} %bitcast.12, f32[27,125]{1,0:T(8,128)} %bitcast.14, ...), custom_call_target="tpu_custom_call" | custom-call | tf_op jit(solution)/shard_map/indicators/pallas_call | solution.py:764
  10.2 0.6 %fusion = (f32[4,512]{1,0:T(4,128)}, f32[4,512]{1,0:T(4,128)}) fusion(f32[8,512]{1,0:T(8,128)S(1)} %indicators.1), kind=kLoop, calls=%fused_computation | loop fusion | bytes 32768 | tf_op jit(solution)/shard_map/slice | solution.py:817
